TPU v7x, 32 devices: a whole 2x2x4 slice. The times are simulated.
32 devices in a mesh: blk: 8 (over z, x), grp: 4 (over y, core).
Axes of the slice: x: 2, y: 2, z: 4, core: 2. Of those that a mesh axis runs over, the one named last changes fastest.
Arguments:
- positions: float32 [3, 2048], P(None, ('blk', 'grp')), may hold values from -0.25 to 31.25, as said below
- moments: float32 [2, 2, 3, 2048], P(None, None, None, ('blk', 'grp')), may hold values from -6 to 6
- inv_polar_re: float32 [2048], P(('blk', 'grp')), may hold values from 0.5 to 2
- inv_polar_im: float32 [2048], P(('blk', 'grp')), may hold values from -0.5 to 0.5
- mode_field: float32 [2, 3, 2048, 512], P(None, None, ('blk', 'grp')), may hold values from -0.078125 to 0.078125
- mode_detune: float32 [512], replicated, may hold values from -1 to 1
- mode_width: float32 [512], replicated, may hold values from 0.05 to 1
Outputs:
- response: float32 [2, 2, 3, 2048], P(None, None, None, ('blk', 'grp'))
Inputs may be any that keep to these rules, and one draw needn't show every extreme that they name: `positions`: dipole n lies within 0.25, in each coordinate, of the lattice site (n % 32, (n // 32) % 32, n // 1024); distinct dipoles are at least 0.5 apart.
All inputs are finite; a program needn't handle non-finite values.
Results may differ from a plain program's by a relative error of at most 0.0003.
Values sent between devices are 32-bit elements; how exact they have to be, the bound alone decides.
No kernel may reach another device: no remote copies, remote signals or barrier semaphores. Data moves between devices by JAX's collectives and lax.ppermute only.
A program may use at most 64 MiB of HBM per device.

v0:
```python
import math

import jax
import jax.numpy as jnp
from jax import lax
from jax.sharding import PartitionSpec as P

wavenumber = 1.0
coupling = 0.05
near_limit = 0.04


def pair_field(deltas, dipoles, axis_sum):
    delta_x, delta_y, delta_z = deltas
    square = delta_x * delta_x + delta_y * delta_y + delta_z * delta_z
    coincide = square < near_limit
    safe_square = jnp.where(coincide, 1.0, square)
    inverse = 1.0 / jnp.sqrt(safe_square)
    phase_arg = wavenumber * safe_square * inverse
    cos_val = jnp.cos(phase_arg)
    sine_val = jnp.sin(phase_arg)
    masked_cube = jnp.where(coincide, 0.0, inverse * inverse * inverse)
    near_re = phase_arg * phase_arg - 1.0
    far_re = 3.0 - phase_arg * phase_arg
    diag_re = (cos_val * near_re - sine_val * phase_arg) * masked_cube
    diag_im = (sine_val * near_re + cos_val * phase_arg) * masked_cube
    scaled = masked_cube / safe_square
    outer_re = (cos_val * far_re + 3.0 * sine_val * phase_arg) * scaled
    outer_im = (sine_val * far_re - 3.0 * cos_val * phase_arg) * scaled
    tile_list = []
    for drive_set in range(len(dipoles) // 6):
        moment_re = dipoles[6 * drive_set : 6 * drive_set + 3]
        moment_im = dipoles[6 * drive_set + 3 : 6 * drive_set + 6]
        proj_re = delta_x * moment_re[0] + delta_y * moment_re[1] + delta_z * moment_re[2]
        proj_im = delta_x * moment_im[0] + delta_y * moment_im[1] + delta_z * moment_im[2]
        along_re = outer_re * proj_re - outer_im * proj_im
        along_im = outer_re * proj_im + outer_im * proj_re
        for component in range(3):
            tile_list.append(
                diag_re * moment_re[component]
                - diag_im * moment_im[component]
                + deltas[component] * along_re
            )
        for component in range(3):
            tile_list.append(
                diag_re * moment_im[component]
                + diag_im * moment_re[component]
                + deltas[component] * along_im
            )
    return jnp.stack([jnp.sum(entry_tile, axis=axis_sum) for entry_tile in tile_list])


def contract(left, right):
    return lax.dot_general(left, right, (((0,), (1,)), ((), ())), precision=lax.Precision.HIGHEST)


def modal_project(mode_rows, moment_rows):
    amp_re = contract(mode_rows[0], moment_rows[:, 0]) - contract(mode_rows[1], moment_rows[:, 1])
    amp_im = contract(mode_rows[0], moment_rows[:, 1]) + contract(mode_rows[1], moment_rows[:, 0])
    return (amp_re, amp_im)


def spread(weights, rows):
    return lax.dot_general(weights, rows, (((0,), (1,)), ((), ())), precision=lax.Precision.HIGHEST)


def modal_spread(mode_rows, amp_re, amp_im, mode_detune, mode_width):
    denominator = mode_detune * mode_detune + mode_width * mode_width
    resp_re = (mode_detune / denominator)[:, None]
    resp_im = (mode_width / denominator)[:, None]
    weighted_re = resp_re * amp_re - resp_im * amp_im
    weighted_im = resp_re * amp_im + resp_im * amp_re
    out_re = spread(weighted_re, mode_rows[0]) - spread(weighted_im, mode_rows[1])
    out_im = spread(weighted_re, mode_rows[1]) + spread(weighted_im, mode_rows[0])
    return jnp.stack([out_re, out_im], axis=1)


def combine(moments, inv_polar_re, inv_polar_im, pair_part, modal_part):
    drives = moments.shape[0]
    dipole_count = moments.shape[3]
    field_sum = coupling * pair_part.reshape(drives, 2, 3, dipole_count) + modal_part.reshape(
        drives, 2, 3, dipole_count
    )
    moment_re = moments[:, 0]
    moment_im = moments[:, 1]
    resp_re = inv_polar_re * moment_re - inv_polar_im * moment_im - field_sum[:, 0]
    resp_im = inv_polar_re * moment_im + inv_polar_im * moment_re - field_sum[:, 1]
    return jnp.stack([resp_re, resp_im], axis=1)


def on_device(positions, moments, inv_polar_re, inv_polar_im, mode_field, mode_detune, mode_width):
    drives = moments.shape[0]
    dipole_count = positions.shape[1]
    flat_moments = moments.reshape(drives * 6, dipole_count)
    mode_rows = mode_field.reshape(2, 3 * dipole_count, mode_field.shape[3])
    amp_re, amp_im = modal_project(mode_rows, moments.reshape(drives, 2, 3 * dipole_count))
    amp_re, amp_im = lax.psum((amp_re, amp_im), ("blk", "grp"))
    modal_part = modal_spread(mode_rows, amp_re, amp_im, mode_detune, mode_width).reshape(
        drives * 6, dipole_count
    )
    group_pos, group_moments = (
        lax.all_gather(positions, "grp", axis=1, tiled=True),
        lax.all_gather(flat_moments, "grp", axis=1, tiled=True),
    )
    initial = jnp.zeros((drives * 6, dipole_count), jnp.float32)
    places = lax.all_gather(group_pos, "blk", axis=1, tiled=True)
    dipoles = lax.all_gather(group_moments, "blk", axis=1, tiled=True)
    columns = places.shape[1]
    block_width = math.gcd(columns, 2048)

    def advance(block, inner):
        source_pos = lax.dynamic_slice_in_dim(places, block * block_width, block_width, 1)
        source_mom = lax.dynamic_slice_in_dim(dipoles, block * block_width, block_width, 1)
        deltas = [positions[axis_c][:, None] - source_pos[axis_c][None, :] for axis_c in range(3)]
        return inner + pair_field(
            deltas, [source_mom[member][None, :] for member in range(drives * 6)], 1
        )

    pair_part = lax.fori_loop(0, columns // block_width, advance, initial)
    return combine(moments, inv_polar_re, inv_polar_im, pair_part, modal_part)


def solution(mesh):
    placed = (
        P(None, ("blk", "grp")),
        P(None, None, None, ("blk", "grp")),
        P(("blk", "grp")),
        P(("blk", "grp")),
        P(None, None, ("blk", "grp"), None),
        P(),
        P(),
    )
    return jax.shard_map(
        on_device,
        mesh=mesh,
        in_specs=placed,
        out_specs=P(None, None, None, ("blk", "grp")),
        check_vma=False,
    )
```

profile of v0, /device:TPU:0, one launch (start us, length us, event | category | flops | bytes accessed | tf_op | source)
XLA Modules:
  0.0 126.5 jit_solution(16070612129556951673)
XLA Ops:
  0.0 0.0 copy-start.1
  0.0 1.2 fusion.63
  1.2 0.0 copy-done.1
  1.2 0.1 reshape.26
  1.3 0.3 fusion.53
  1.6 0.3 convolution_subtract_fusion
  1.9 0.3 fusion.49
  2.3 0.3 convolution_add_fusion
  2.6 0.0 copy-start.3
  2.6 42.1 %all-reduce = (f32[512,2]{0,1:T(2,128)S(1)}, f32[512,2]{0,1:T(2,128)S(1)}) all-reduce(f32[512,2]{0,1:T(2,128)S(1)} %convolution_add_fusion, f32[512,2]{0,1:T(2,128)S(1)} %convolution_subtract_fusion), channel_id=1, replica_groups=mesh['blk'=8,'grp'=4] {'blk','grp'}, use_global_device_ids=true, to_apply=%region_13.0 | all-reduce | flops 2048 | bytes 16384 | tf_op jit(solution)/shard_map/psum | solution.py:97
  44.7 0.0 copy-start.2
  44.7 0.0 copy-done.3
  44.7 0.7 copy-done.2
  45.4 0.4 fusion.62
  45.8 0.4 convolution_subtract_fusion.1
  46.2 0.1 stack.79
  46.3 0.4 fusion.61
  46.7 0.4 convolution_add_fusion.1
  47.1 0.1 stack.80
  47.2 5.5 %all-gather.1 = f32[4,64,12]{1,2,0:T(8,128)S(1)} all-gather(f32[1,64,12]{1,2,0:T(8,128)S(1)} %bitcast.76), channel_id=1, replica_groups=mesh['blk'=8,'grp'=4] {'grp'}, dimensions={0}, use_global_device_ids=true | all-gather | bytes 15360 | tf_op jit(solution)/shard_map/all_gather | solution.py:103
  52.8 0.1 reshape.30
  52.9 30.5 %all_gather.15 = f32[12,2048]{1,0:T(8,128)S(1)} all-gather(f32[12,256]{1,0:T(8,128)S(1)} %bitcast.75), channel_id=1, replica_groups=mesh['blk'=8,'grp'=4] {'blk'}, dimensions={1}, use_global_device_ids=true | all-gather | bytes 110592 | tf_op jit(solution)/shard_map/all_gather | solution.py:107
  83.4 0.1 fusion.64
  83.4 0.0 copy-start
  83.5 0.7 copy-done
  84.1 5.2 %all-gather = f32[4,64,3]{1,2,0:T(4,128)S(1)} all-gather(f32[1,64,3]{1,2,0:T(4,128)S(1)} %bitcast.95), channel_id=1, replica_groups=mesh['blk'=8,'grp'=4] {'grp'}, dimensions={0}, use_global_device_ids=true | all-gather | bytes 3840 | tf_op jit(solution)/shard_map/all_gather | solution.py:102
  89.3 0.1 reshape.28
  89.4 30.6 %all_gather.13 = f32[3,2048]{1,0:T(4,128)S(1)} all-gather(f32[3,256]{1,0:T(4,128)S(1)} %bitcast.77), channel_id=1, replica_groups=mesh['blk'=8,'grp'=4] {'blk'}, dimensions={1}, use_global_device_ids=true | all-gather | bytes 27648 | tf_op jit(solution)/shard_map/all_gather | solution.py:106
  120.0 5.1 %fusion.45 = (f32[64]{0:T(128)S(1)}, f32[64]{0:T(128)S(1)}, f32[64]{0:T(128)S(1)}, f32[64]{0:T(128)S(1)}, f32[64]{0:T(128)S(1)}, /*index=5*/f32[64]{0:T(128)S(1)...) fusion(f32[2048]{0:T(1024)S(1)} %bitcast.81, ...), kind=kLoop, calls=%fused_computation.80 | loop fusion | flops 18349312 | bytes 126720 | tf_op jit(solution)/shard_map/while/body/eval_jaxpr/reduce_sum | solution.py:50
  125.2 0.0 copy-start.4
  125.2 0.0 copy-start.5
  125.2 0.6 copy-done.4
  125.9 0.0 copy-done.5
  125.9 0.6 copy.37
  (14 shorter events, 0.2 us)
Async XLA Ops:
  0.0 1.2 copy-start.1
  2.6 42.1 %copy-start.3 = (f32[512]{0:T(512)S(1)}, f32[512]{0:T(512)}, u32[]{:S(2)}) copy-start(f32[512]{0:T(512)} %param.13) | copy-start | bytes 6148
  44.7 0.7 copy-start.2
  83.4 0.7 copy-start
  125.2 0.7 copy-start.4
  125.2 0.7 copy-start.5
where the time goes:
time: 127 us; the launch traced here: 126 us
  blocking collectives  114 us (90%)
  other arithmetic  5.14 us (4%)
  local copies, waits for them, and re-layouts  4.42 us (3%)
  matrix products  2.95 us (2%)
    psum x1, blocking collectives, on_device(): amp_re, amp_im = lax.psum((amp_re, amp_im), ('blk', 'grp'))  42.1 us
    all_gather x1, blocking collectives, on_device(): places = lax.all_gather(group_pos, 'blk', axis=1, tiled=True)  30.6 us
    all_gather x1, blocking collectives, on_device(): dipoles = lax.all_gather(group_moments, 'blk', axis=1, tiled=True)  30.5 us
    all_gather x1, blocking collectives, on_device(): lax.all_gather(flat_moments, 'grp', axis=1, tiled=True)  5.52 us
    all_gather x1, blocking collectives, on_device(): lax.all_gather(positions, 'grp', axis=1, tiled=True)  5.18 us
    reduce_sum x1, other arithmetic, pair_field(): jnp.sum(entry_tile, axis=axis_sum)  5.11 us

commit v1 on v0

v1 whole, which is shorter than its diff:
```python
import functools
import math

import jax
import jax.numpy as jnp
from jax import lax
from jax.experimental import pallas as pl
from jax.experimental.pallas import tpu as pltpu
from jax.sharding import PartitionSpec as P

wavenumber = 1.0
coupling = 0.05
near_limit = 0.04

AXES = ("blk", "grp")
LANES = 128
ROWS = 16
CHUNK = 2 * LANES

PI_HIGH = 3.140625
PI_LOW = math.pi - PI_HIGH
SIN_POLY = (-0.16666656732559204, 0.008332998491823673, -0.00019805235206149518, 2.5970118713303236e-06)
COS_POLY = (-0.4999992549419403, 0.04166382923722267, -0.0013854617718607187, 2.316308928129729e-05)


def horner(coefficients, value):
    total = jnp.full_like(value, coefficients[-1])
    for entry in coefficients[-2::-1]:
        total = total * value + entry
    return total


def green_terms(delta_x, delta_y, delta_z):
    square = delta_x * delta_x + delta_y * delta_y + delta_z * delta_z
    coincide = square < near_limit
    square = jnp.where(coincide, 1.0, square)
    inverse = lax.rsqrt(square)
    radius = square * inverse
    half_turns = jnp.floor(radius * (1.0 / math.pi) + 0.5)
    angle = (radius - half_turns * PI_HIGH) - half_turns * PI_LOW
    angle_sq = angle * angle
    sine = angle + angle * (angle_sq * horner(SIN_POLY, angle_sq))
    cosine = 1.0 + angle_sq * horner(COS_POLY, angle_sq)
    odd = (half_turns.astype(jnp.int32) & 1) == 1
    inverse_sq = inverse * inverse
    cube = inverse_sq * inverse
    cube = jnp.where(odd, -cube, cube)
    cube = jnp.where(coincide, 0.0, cube)
    fifth = cube * inverse_sq
    near = square - 1.0
    far = 3.0 - square
    sine_r = sine * radius
    cosine_r = cosine * radius
    return (
        (cosine * near - sine_r) * cube,
        (sine * near + cosine_r) * cube,
        (cosine * far + 3.0 * sine_r) * fifth,
        (sine * far - 3.0 * cosine_r) * fifth,
    )


def split(value):
    high = value.astype(jnp.bfloat16)
    return high, (value - high.astype(jnp.float32)).astype(jnp.bfloat16)


def dot_t(left, right):
    return lax.dot_general(left, right, (((1,), (1,)), ((), ())), preferred_element_type=jnp.float32)


def project_kernel(left_ref, mode_ref, amp_ref, high_ref, low_ref):
    mode_high, mode_low = split(mode_ref[...])
    high_ref[...] = mode_high
    low_ref[...] = mode_low
    left_high, left_low = split(left_ref[...])
    both = jnp.dot(jnp.concatenate([left_high, left_low], axis=0), mode_high, preferred_element_type=jnp.float32)
    amp = both[0:4] + both[4:8] + jnp.dot(left_high, mode_low, preferred_element_type=jnp.float32)
    for tile in range(amp.shape[1] // LANES):
        amp_ref[4 * tile : 4 * tile + 4, :] = amp[:, tile * LANES : (tile + 1) * LANES]


def pair_kernel(chips, centre_ref, target_ref, source_ref, out_ref, green_ref):
    targets = target_ref.shape[1]
    out_ref[...] = jnp.zeros_like(out_ref)
    centre = [centre_ref[axis_c] for axis_c in range(3)]

    def chunk(step):
        base = step * (2 * ROWS)
        if not isinstance(base, int):
            base = pl.multiple_of(base, 2 * ROWS)
        block = jnp.concatenate(
            [source_ref[pl.ds(base, ROWS), :], source_ref[pl.ds(base + ROWS, ROWS), :]], axis=1
        )
        place = [block[12 + axis_c : 13 + axis_c, :] for axis_c in range(3)]
        for group in range(targets // 8):
            for half in range(CHUNK // LANES):
                lanes = slice(half * LANES, (half + 1) * LANES)
                rows = slice(group * 8, group * 8 + 8)
                deltas = [
                    target_ref[axis_c, rows, :] - jnp.broadcast_to(place[axis_c][:, lanes], (8, LANES))
                    for axis_c in range(3)
                ]
                for part, tile in enumerate(green_terms(*deltas)):
                    green_ref[part * targets + group * 8 : part * targets + group * 8 + 8, lanes] = tile
        local = [place[axis_c] - centre[axis_c] for axis_c in range(3)]
        moment = [block[4 * axis_c : 4 * axis_c + 4, :] for axis_c in range(3)]
        along = moment[0] * local[0] + moment[1] * local[1] + moment[2] * local[2]
        features = jnp.concatenate(
            [block]
            + [block * local[axis_c] for axis_c in range(3)]
            + [along * local[axis_c] for axis_c in range(3)]
            + [jnp.zeros_like(along)],
            axis=0,
        )
        out_ref[...] += lax.dot_general(
            features,
            green_ref[...],
            (((1,), (1,)), ((), ())),
            precision=lax.Precision.HIGHEST,
            preferred_element_type=jnp.float32,
        )

    steps = chips // 2
    if steps <= 4:
        for step in range(steps):
            chunk(step)
    else:
        pl.loop(0, steps)(chunk)


def finish_kernel(
    amp_ref, high_ref, low_ref, detune_ref, width_ref, first_ref, second_ref, centre_ref, place_ref, moment_ref,
    polar_re_ref, polar_im_ref, out_ref,
):
    targets = place_ref.shape[1]
    tiles = detune_ref.shape[1] // LANES
    amp = jnp.concatenate([amp_ref[4 * tile : 4 * tile + 4, :] for tile in range(tiles)], axis=1)
    detune, width = detune_ref[...], width_ref[...]
    denominator = detune * detune + width * width
    resp_re, resp_im = detune / denominator, width / denominator
    weighted = []
    for drive in range(2):
        amp_re, amp_im = amp[2 * drive : 2 * drive + 1], amp[2 * drive + 1 : 2 * drive + 2]
        weighted += [resp_re * amp_re - resp_im * amp_im, resp_re * amp_im + resp_im * amp_re]
    weight_high, weight_low = split(jnp.concatenate(weighted, axis=0))
    both = dot_t(jnp.concatenate([weight_high, weight_low], axis=0), high_ref[...])
    modal = both[0:4] + both[4:8] + dot_t(weight_high, low_ref[...])

    raw = first_ref[...] + second_ref[...]
    near_re, near_im, far_re, far_im = [raw[:, part * targets : (part + 1) * targets] for part in range(4)]
    local = [place_ref[axis_c : axis_c + 1, :] - centre_ref[axis_c] for axis_c in range(3)]

    def rows_of(table, group, axis_c):
        start = group * ROWS + 4 * axis_c
        return table[start : start + 4]

    def combine_parts(real, imag):
        out = []
        for drive in range(2):
            out.append(real[2 * drive : 2 * drive + 1] - imag[2 * drive + 1 : 2 * drive + 2])
            out.append(real[2 * drive + 1 : 2 * drive + 2] + imag[2 * drive : 2 * drive + 1])
        return jnp.concatenate(out, axis=0)

    def outer(table, axis_c):
        straight = sum(local[j] * rows_of(table, 0, j) for j in range(3))
        dotted = sum(rows_of(table, 1 + j, j) for j in range(3))
        crossed = sum(local[j] * rows_of(table, 1 + axis_c, j) for j in range(3))
        return local[axis_c] * (straight - dotted) - crossed + rows_of(table, 4, axis_c)

    half = 3 * targets
    for axis_c in range(3):
        real = rows_of(near_re, 0, axis_c) + outer(far_re, axis_c)
        imag = rows_of(near_im, 0, axis_c) + outer(far_im, axis_c)
        pair = combine_parts(real, imag)
        mode_re = modal[:, axis_c * targets : (axis_c + 1) * targets]
        mode_im = modal[:, half + axis_c * targets : half + (axis_c + 1) * targets]
        field = coupling * pair + combine_parts(mode_re, mode_im)
        polar_re, polar_im = polar_re_ref[...], polar_im_ref[...]
        for drive in range(2):
            moment_re = moment_ref[drive, axis_c, 0:1, :]
            moment_im = moment_ref[drive, axis_c, 1:2, :]
            out_ref[drive, axis_c, 0:1, :] = (
                polar_re * moment_re - polar_im * moment_im - field[2 * drive : 2 * drive + 1]
            )
            out_ref[drive, axis_c, 1:2, :] = (
                polar_re * moment_im + polar_im * moment_re - field[2 * drive + 1 : 2 * drive + 2]
            )


def in_vmem(count):
    return [pl.BlockSpec(memory_space=pltpu.VMEM)] * count


def in_smem():
    return pl.BlockSpec(memory_space=pltpu.SMEM)


def on_device(devices, positions, moments, inv_polar_re, inv_polar_im, mode_field, mode_detune, mode_width):
    targets = positions.shape[1]
    modes = mode_field.shape[3]
    shape = jax.ShapeDtypeStruct

    def exchange(value, distance):
        return lax.ppermute(value, AXES, [(i, i ^ distance) for i in range(devices)])

    ordered = jnp.transpose(moments, (2, 0, 1, 3)).reshape(12, targets)
    own = jnp.concatenate([ordered, positions, jnp.zeros((1, targets), jnp.float32)], axis=0)
    other = exchange(own, 1)

    flat = moments.reshape(2, 2, 3 * targets)
    swapped = jnp.stack([-flat[:, 1], flat[:, 0]], axis=1)
    left = jnp.concatenate([flat, swapped], axis=2).reshape(4, 6 * targets)
    amp, mode_high, mode_low = pl.pallas_call(
        project_kernel,
        out_shape=(
            shape((4 * modes // LANES, LANES), jnp.float32),
            shape((6 * targets, modes), jnp.bfloat16),
            shape((6 * targets, modes), jnp.bfloat16),
        ),
        in_specs=in_vmem(2),
        out_specs=tuple(in_vmem(3)),
        cost_estimate=pl.CostEstimate(flops=2_000_000, bytes_accessed=1_600_000, transcendentals=0),
        name="project",
    )(left, mode_field.reshape(6 * targets, modes))

    centre = jnp.mean(positions, axis=1)
    target_cols = jnp.broadcast_to(positions[:, :, None], (3, targets, LANES))

    def pair(sources, chips):
        return pl.pallas_call(
            functools.partial(pair_kernel, chips),
            out_shape=shape((5 * ROWS, 4 * targets), jnp.float32),
            in_specs=[in_smem()] + in_vmem(2),
            out_specs=in_vmem(1)[0],
            scratch_shapes=[pltpu.VMEM((4 * targets, CHUNK), jnp.float32)],
            cost_estimate=pl.CostEstimate(
                flops=2 * 5 * ROWS * 4 * targets * chips * LANES, bytes_accessed=400_000, transcendentals=0
            ),
            name="pair",
        )(centre, target_cols, sources)

    gathered = jnp.concatenate([own, other], axis=1)
    distance = devices // 2
    first = None
    while distance > 1:
        chips = gathered.shape[0] // ROWS
        arrived = exchange(jnp.concatenate([gathered, amp], axis=0), distance)
        last = distance == 2
        if last:
            first = pair(gathered, chips)
        amp = amp + arrived[chips * ROWS :]
        if last:
            second = pair(arrived, chips)
        else:
            gathered = jnp.concatenate([gathered, arrived[: chips * ROWS]], axis=0)
        distance //= 2
    amp = amp + exchange(amp, 1)

    out = pl.pallas_call(
        finish_kernel,
        out_shape=shape((2, 3, 2, targets), jnp.float32),
        in_specs=in_vmem(7) + [in_smem()] + in_vmem(4),
        out_specs=in_vmem(1)[0],
        cost_estimate=pl.CostEstimate(flops=2_000_000, bytes_accessed=1_000_000, transcendentals=0),
        name="finish",
    )(
        amp,
        mode_high,
        mode_low,
        mode_detune[None],
        mode_width[None],
        first,
        second,
        centre,
        positions,
        jnp.transpose(moments, (0, 2, 1, 3)),
        inv_polar_re[None],
        inv_polar_im[None],
    )
    return jnp.transpose(out, (0, 2, 1, 3))


def solution(mesh):
    placed = (
        P(None, AXES),
        P(None, None, None, AXES),
        P(AXES),
        P(AXES),
        P(None, None, AXES, None),
        P(),
        P(),
    )
    return jax.shard_map(
        functools.partial(on_device, mesh.size),
        mesh=mesh,
        in_specs=placed,
        out_specs=P(None, None, None, AXES),
        check_vma=False,
    )
```

time: 127 us -> 35 us (0.28)
  blocking collectives: 114 us -> 0 us
  Pallas kernels: 0 us -> 10.7 us
  starting transfers between devices: 0 us -> 10.5 us
  waiting for transfers between devices: 0 us -> 7.32 us
  matrix products: 2.95 us -> 0 us
  local copies, waits for them, and re-layouts: 4.42 us -> 2.42 us
  other arithmetic: 5.14 us -> 3.71 us
    all_gather x4 -> x0, blocking collectives: 71.8 us -> none  [the longest x1 30.6 us: on_device(): places = lax.all_gather(group_pos, 'blk', axis=1, tiled=True)]
    psum x1 -> x0, blocking collectives: 42.1 us -> none  [on_device(): amp_re, amp_im = lax.psum((amp_re, amp_im), ('blk', 'grp'))]
    pallas_call x0 -> x4, Pallas kernels: none -> 10.7 us  [the longest x2 6.24 us: pair(): pl.pallas_call(functools.partial(pair_kernel, chips), out_shape=shape((5...]
    ppermute x0 -> x6, starting transfers between devices: none -> 10.5 us  [exchange(): lax.ppermute(value, AXES, [(i, i ^ distance) for i in range(devices)])]
    ppermute x0 -> x6, waiting for transfers between devices: none -> 7.32 us  [exchange(): lax.ppermute(value, AXES, [(i, i ^ distance) for i in range(devices)])]
    reduce_sum x1, other arithmetic: 5.11 us -> 0.12 us  [on_device(): centre = jnp.mean(positions, axis=1)]
    dot_general x8 -> x0, matrix products: 2.95 us -> none  [the longest x4 1.66 us: spread(): lax.dot_general(weights, rows, (((0,), (1,)), ((), ())), precision=lax.Pr...]
    concatenate x0 -> x7, other arithmetic: none -> 2.31 us  [the longest x4 0.93 us: on_device(): arrived = exchange(jnp.concatenate([gathered, amp], axis=0), distance)]
  transfers between devices with their start and end apart: 0 -> 6, of which waited for: 0 -> 4; matrix products, arithmetic and copies ran while one was open for 0% -> 9% of each run, Pallas kernels for 0% -> 24%
where the time goes in v1:
time: 35 us; the launch traced here: 34.7 us
  Pallas kernels  10.7 us (31%)
  starting transfers between devices  10.5 us (30%)
  waiting for transfers between devices  7.32 us (21%)
  other arithmetic  3.71 us (11%)
  local copies, waits for them, and re-layouts  2.42 us (7%)
    ppermute x6, starting transfers between devices, exchange(): lax.ppermute(value, AXES, [(i, i ^ distance) for i in range(devices)])  10.5 us
    ppermute x6, waiting for transfers between devices, exchange(): lax.ppermute(value, AXES, [(i, i ^ distance) for i in range(devices)])  7.32 us
    pallas_call x2, Pallas kernels, pair(): pl.pallas_call(functools.partial(pair_kernel, chips), out_shape=shape((5...  6.24 us
    pallas_call x1, Pallas kernels, on_device(): pl.pallas_call(finish_kernel, out_shape=shape((2, 3, 2, targets), jnp.flo...  2.32 us
    pallas_call x1, Pallas kernels, on_device(): pl.pallas_call(project_kernel, out_shape=(shape((4 * modes // LANES, LANE...  2.1 us
    concatenate x4, other arithmetic, on_device(): arrived = exchange(jnp.concatenate([gathered, amp], axis=0), distance)  0.93 us
    unnamed x9, local copies, waits for them, and re-layouts  0.79 us
    broadcast_in_dim x1, local copies, waits for them, and re-layouts, on_device(): target_cols = jnp.broadcast_to(positions[:, :, None], (3, targets, LANES))  0.73 us
  transfers between devices with their start and end apart: 6, of which 4 were waited for; matrix products, arithmetic and copies ran while one was open for 9% of the time, Pallas kernels for 24%

profile of v1, /device:TPU:0, one launch (start us, length us, event | category | flops | bytes accessed | tf_op | source)
XLA Modules:
  0.0 34.7 jit_solution(11139416877429881824)
XLA Ops:
  0.0 0.7 %copy.12 = f32[3,2,2,64]{3,2,1,0:T(2,128)S(1)} copy(f32[3,2,2,64]{3,2,0,1:T(2,128)} %bitcast.9) | data formatting | bytes 6144 | tf_op jit(solution)/shard_map/transpose | solution.py:206
  0.7 0.0 copy-start
  0.7 0.7 %copy-done = f32[3,64]{1,0:T(4,128)S(1)} copy-done((f32[3,64]{1,0:T(4,128)S(1)}, f32[3,64]{1,0:T(4,128)}, u32[]{:S(2)}) %copy-start) | copy-done | bytes 792
  1.4 0.0 copy-start.2
  1.4 0.6 %collective-permute-start = (f32[16,64]{1,0:T(8,128)S(1)}, f32[16,64]{1,0:T(8,128)S(1)}, u32[]{:S(2)}, u32[]{:S(2)}) collective-permute-start(f32[16,64]{1,0:T(8,128)S(1)} %pad_maximum_fusion.4), channel_id=1, source_target_pairs={{0,1},{1,0},{2,3},{3,2},{4,5},{5,4},{6,7},{7,6},{8,9},{9,8},{10,11... | collective-permute-start | bytes 12296 | tf_op jit(solution)/shard_map/ppermute | solution.py:204
  1.9 0.1 copy-done.2
  2.1 0.1 reshape.14
  2.2 0.1 concatenate.36
  2.3 0.7 %pad_maximum_fusion.5.left_ref = f32[4,384]{1,0:T(4,128)} fusion(f32[4,192]{1,0:T(4,128)S(1)} %concatenate.37, f32[4,192]{1,0:T(4,128)S(1)} %concatenate.36), kind=kLoop, calls=%fused_computation.14 | loop fusion | flops 1536 | bytes 12288 | tf_op jit(solution)/shard_map/concatenate | solution.py:212
  2.9 2.1 %project.1 = (f32[16,128]{1,0:T(8,128)}, bf16[384,512]{1,0:T(8,128)(2,1)}, bf16[384,512]{1,0:T(8,128)(2,1)}) custom-call(f32[4,384]{1,0:T(4,128)} %pad_maximum_fusion.5.left_ref, f32[384,512]{1,0:T(8,128)} %bitcast.8), custom_call_target="tpu_custom_call" | custom-call | flops 2000000 | bytes 1600000 | tf_op jit(solution)/shard_map/project/pallas_call | solution.py:213
  5.0 0.0 collective-permute-done
  5.0 0.8 %pad_maximum_fusion.3 = f32[32,128]{1,0:T(8,128)S(1)} fusion(f32[16,128]{1,0:T(8,128)} %get-tuple-element.8, f32[16,64]{1,0:T(8,128)S(1)} %collective-permute-done, f32[1,64]{1,0:T(1,128)S(1)} %broadcast_in_dim.21, f32[3,64]{1,0:T(4,128)S(1)} %copy-done, f32[12,64]{1,0:T(8,128)S(1)} %reshape.16), kind=kLoop, calls=%fused_computation.3 | loop fusion | flops 16384 | bytes 32768 | tf_op jit(solution)/shard_map/concatenate | solution.py:247
  5.8 0.0 copy-start.3
  5.8 4.1 %collective-permute-start.1 = (f32[32,128]{1,0:T(8,128)S(1)}, f32[32,128]{1,0:T(8,128)S(1)}, u32[]{:S(2)}, u32[]{:S(2)}) collective-permute-start(f32[32,128]{1,0:T(8,128)S(1)} %pad_maximum_fusion.3), channel_id=1, source_target_pairs={{0,16},{1,17},{2,18},{3,19},{4,20},{5,21},{6,22},{7,23},{8,24},{9,... | collective-permute-start | bytes 49160 | tf_op jit(solution)/shard_map/ppermute | solution.py:204
  9.9 0.1 constant_dynamic-update-slice_fusion.4
  10.0 1.6 %collective-permute-done.1 = f32[32,128]{1,0:T(8,128)S(1)} collective-permute-done((f32[32,128]{1,0:T(8,128)S(1)}, f32[32,128]{1,0:T(8,128)S(1)}, u32[]{:S(2)}, u32[]{:S(2)}) %collective-permute-start.1) | collective-permute-done | bytes 16416 | tf_op jit(solution)/shard_map/ppermute | solution.py:204
  11.6 0.0 copy-done.3
  11.6 0.1 pad_maximum_fusion.2
  11.7 1.9 %collective-permute-start.2 = (f32[48,128]{1,0:T(8,128)S(1)}, f32[48,128]{1,0:T(8,128)S(1)}, u32[]{:S(2)}, u32[]{:S(2)}) collective-permute-start(f32[48,128]{1,0:T(8,128)S(1)} %pad_maximum_fusion.2), channel_id=1, source_target_pairs={{0,8},{1,9},{2,10},{3,11},{4,12},{5,13},{6,14},{7,15},{8,0},{9,1},... | collective-permute-start | bytes 73736 | tf_op jit(solution)/shard_map/ppermute | solution.py:204
  13.6 1.9 %collective-permute-done.2 = f32[48,128]{1,0:T(8,128)S(1)} collective-permute-done((f32[48,128]{1,0:T(8,128)S(1)}, f32[48,128]{1,0:T(8,128)S(1)}, u32[]{:S(2)}, u32[]{:S(2)}) %collective-permute-start.2) | collective-permute-done | bytes 24608 | tf_op jit(solution)/shard_map/ppermute | solution.py:204
  15.5 0.1 pad_maximum_fusion.1
  15.6 1.9 %collective-permute-start.3 = (f32[80,128]{1,0:T(8,128)S(1)}, f32[80,128]{1,0:T(8,128)S(1)}, u32[]{:S(2)}, u32[]{:S(2)}) collective-permute-start(f32[80,128]{1,0:T(8,128)S(1)} %pad_maximum_fusion.1), channel_id=1, source_target_pairs={{0,4},{1,5},{2,6},{3,7},{4,0},{5,1},{6,2},{7,3},{8,12},{9,13},{10,... | collective-permute-start | bytes 122888 | tf_op jit(solution)/shard_map/ppermute | solution.py:204
  17.6 0.1 reduce_sum.9
  17.7 1.9 %collective-permute-done.3 = f32[80,128]{1,0:T(8,128)S(1)} collective-permute-done((f32[80,128]{1,0:T(8,128)S(1)}, f32[80,128]{1,0:T(8,128)S(1)}, u32[]{:S(2)}, u32[]{:S(2)}) %collective-permute-start.3) | collective-permute-done | bytes 40992 | tf_op jit(solution)/shard_map/ppermute | solution.py:204
  19.6 2.0 %collective-permute-start.4 = (f32[144,128]{1,0:T(8,128)S(1)}, f32[144,128]{1,0:T(8,128)S(1)}, u32[]{:S(2)}, u32[]{:S(2)}) collective-permute-start(f32[144,128]{1,0:T(8,128)S(1)} %constant_dynamic-update-slice_fusion), channel_id=1, source_target_pairs={{0,2},{1,3},{2,0},{3,1},{4,6},{5,7},{6,4},{7,5},{8,10},{9,11},{10,... | collective-permute-start | bytes 221192 | tf_op jit(solution)/shard_map/ppermute | solution.py:204
  21.7 0.6 %broadcast_multiply_fusion.centre_ref = f32[3]{0:T(128)} fusion(f32[3]{0:T(128)S(1)} %reduce_sum.9), kind=kLoop, calls=%fused_computation.17 | loop fusion | flops 3 | bytes 24 | tf_op jit(solution)/shard_map/div | solution.py:226
  22.3 1.8 %collective-permute-done.4.source_ref = f32[144,128]{1,0:T(8,128)S(1)} collective-permute-done((f32[144,128]{1,0:T(8,128)S(1)}, f32[144,128]{1,0:T(8,128)S(1)}, u32[]{:S(2)}, u32[]{:S(2)}) %collective-permute-start.4) | collective-permute-done | bytes 73760 | tf_op jit(solution)/shard_map/ppermute | solution.py:204
  24.1 0.0 copy-start.1
  24.1 0.0 collective-permute-start.5
  24.1 0.7 %pad_maximum_fusion.source_ref = f32[128,128]{1,0:T(8,128)} fusion(f32[64,128]{1,0:T(8,128)S(1)} %get-tuple-element.11, f32[32,128]{1,0:T(8,128)S(1)} %get-tuple-element.13, f32[16,128]{1,0:T(8,128)S(1)} %get-tuple-element.15, f32[16,64]{1,0:T(8,128)S(1)} %collective-permute-done, f32[1,64]{1,0:T(1,128)S(1)} %broadcast_in_dim.21, f32[3,64]{1,0:T(4,128)S(1)} %copy-done, ...), kind=kLoop, calls=%fused_computation | loop fusion | flops 98304 | bytes 131072 | tf_op jit(solution)/shard_map/concatenate | solution.py:255
  24.8 0.0 copy-done.1
  24.8 0.7 %broadcast_in_dim.24.target_ref = f32[3,64,128]{2,1,0:T(8,128)} broadcast(f32[3,64]{1,0:T(4,128)S(1)} %copy-done), dimensions={0,1} | broadcast | bytes 99072 | tf_op jit(solution)/shard_map/broadcast_in_dim | solution.py:227
  25.5 3.1 %pair.2.first_ref = f32[80,256]{1,0:T(8,128)} custom-call(f32[3]{0:T(128)} %broadcast_multiply_fusion.centre_ref, f32[3,64,128]{2,1,0:T(8,128)} %broadcast_in_dim.24.target_ref, f32[128,128]{1,0:T(8,128)} %pad_maximum_fusion.source_ref), custom_call_target="tpu_custom_call" | custom-call | flops 41943040 | bytes 400000 | tf_op jit(solution)/shard_map/pair/pallas_call | solution.py:230
  28.6 3.1 %pair.3.second_ref = f32[80,256]{1,0:T(8,128)} custom-call(f32[3]{0:T(128)} %broadcast_multiply_fusion.centre_ref, f32[3,64,128]{2,1,0:T(8,128)} %broadcast_in_dim.24.target_ref, f32[144,128]{1,0:T(8,128)} %copy-done.1), custom_call_target="tpu_custom_call" | custom-call | flops 41943040 | bytes 400000 | tf_op jit(solution)/shard_map/pair/pallas_call | solution.py:230
  31.7 0.0 collective-permute-done.5
  31.8 0.6 %add.19.amp_ref = f32[16,128]{1,0:T(8,128)} add(f32[16,128]{1,0:T(8,128)S(1)} %slice_add_fusion, f32[16,128]{1,0:T(8,128)S(1)} %collective-permute-done.5) | non-fusion elementwise | flops 2048 | bytes 24576 | tf_op jit(solution)/shard_map/add | solution.py:257
  32.3 2.3 %finish.1 = f32[2,3,2,64]{3,2,1,0:T(2,128)} custom-call(f32[16,128]{1,0:T(8,128)} %add.19.amp_ref, bf16[384,512]{1,0:T(8,128)(2,1)} %get-tuple-element.9.high_ref, bf16[384,512]{1,0:T(8,128)(2,1)} %get-tuple-element.10.low_ref, f32[1,512]{1,0:T(1,128)} %bitcast.11, f32[1,512]{1,0:T(1,128)} %bitcast.12, f32[80,256]{1,0:T(8,128)} %pair.2.first_ref, ...), custom_call_target="tpu_custom_call" | custom-call | flops 2000000 | bytes 1000000 | tf_op jit(solution)/shard_map/finish/pallas_call | solution.py:259
  (13 shorter events, 0.1 us)
Async XLA Ops:
  0.7 0.7 %copy-start = (f32[3,64]{1,0:T(4,128)S(1)}, f32[3,64]{1,0:T(4,128)}, u32[]{:S(2)}) copy-start(f32[3,64]{1,0:T(4,128)} %place_ref.1) | copy-start | bytes 2308
  1.4 0.7 %copy-start.2 = (f32[2,2,3,64]{3,1,2,0:T(2,128)S(1)}, f32[2,2,3,64]{3,1,2,0:T(2,128)}, u32[]{:S(2)}) copy-start(f32[2,2,3,64]{3,1,2,0:T(2,128)} %param.8) | copy-start | bytes 9220
  1.4 3.7 %collective-permute-start = (f32[16,64]{1,0:T(8,128)S(1)}, f32[16,64]{1,0:T(8,128)S(1)}, u32[]{:S(2)}, u32[]{:S(2)}) collective-permute-start(f32[16,64]{1,0:T(8,128)S(1)} %pad_maximum_fusion.4), channel_id=1, source_target_pairs={{0,1},{1,0},{2,3},{3,2},{4,5},{5,4},{6,7},{7,6},{8,9},{9,8},{10,11... | collective-permute-start | bytes 12296 | tf_op jit(solution)/shard_map/ppermute | solution.py:204
  5.8 5.8 %copy-start.3 = (f32[16,128]{1,0:T(8,128)S(1)}, f32[16,128]{1,0:T(8,128)}, u32[]{:S(2)}) copy-start(f32[16,128]{1,0:T(8,128)} %get-tuple-element.8) | copy-start | bytes 24580
  5.8 5.8 %collective-permute-start.1 = (f32[32,128]{1,0:T(8,128)S(1)}, f32[32,128]{1,0:T(8,128)S(1)}, u32[]{:S(2)}, u32[]{:S(2)}) collective-permute-start(f32[32,128]{1,0:T(8,128)S(1)} %pad_maximum_fusion.3), channel_id=1, source_target_pairs={{0,16},{1,17},{2,18},{3,19},{4,20},{5,21},{6,22},{7,23},{8,24},{9,... | collective-permute-start | bytes 49160 | tf_op jit(solution)/shard_map/ppermute | solution.py:204
  11.7 3.8 %collective-permute-start.2 = (f32[48,128]{1,0:T(8,128)S(1)}, f32[48,128]{1,0:T(8,128)S(1)}, u32[]{:S(2)}, u32[]{:S(2)}) collective-permute-start(f32[48,128]{1,0:T(8,128)S(1)} %pad_maximum_fusion.2), channel_id=1, source_target_pairs={{0,8},{1,9},{2,10},{3,11},{4,12},{5,13},{6,14},{7,15},{8,0},{9,1},... | collective-permute-start | bytes 73736 | tf_op jit(solution)/shard_map/ppermute | solution.py:204
  15.6 4.0 %collective-permute-start.3 = (f32[80,128]{1,0:T(8,128)S(1)}, f32[80,128]{1,0:T(8,128)S(1)}, u32[]{:S(2)}, u32[]{:S(2)}) collective-permute-start(f32[80,128]{1,0:T(8,128)S(1)} %pad_maximum_fusion.1), channel_id=1, source_target_pairs={{0,4},{1,5},{2,6},{3,7},{4,0},{5,1},{6,2},{7,3},{8,12},{9,13},{10,... | collective-permute-start | bytes 122888 | tf_op jit(solution)/shard_map/ppermute | solution.py:204
  19.6 4.4 %collective-permute-start.4 = (f32[144,128]{1,0:T(8,128)S(1)}, f32[144,128]{1,0:T(8,128)S(1)}, u32[]{:S(2)}, u32[]{:S(2)}) collective-permute-start(f32[144,128]{1,0:T(8,128)S(1)} %constant_dynamic-update-slice_fusion), channel_id=1, source_target_pairs={{0,2},{1,3},{2,0},{3,1},{4,6},{5,7},{6,4},{7,5},{8,10},{9,11},{10,... | collective-permute-start | bytes 221192 | tf_op jit(solution)/shard_map/ppermute | solution.py:204
  24.1 0.7 %copy-start.1 = (f32[144,128]{1,0:T(8,128)}, f32[144,128]{1,0:T(8,128)S(1)}, u32[]{:S(2)}) copy-start(f32[144,128]{1,0:T(8,128)S(1)} %collective-permute-done.4.source_ref) | copy-start | bytes 221188
  24.1 7.7 %collective-permute-start.5 = (f32[16,128]{1,0:T(8,128)S(1)}, f32[16,128]{1,0:T(8,128)S(1)}, u32[]{:S(2)}, u32[]{:S(2)}) collective-permute-start(f32[16,128]{1,0:T(8,128)S(1)} %slice_add_fusion), channel_id=1, source_target_pairs={{0,1},{1,0},{2,3},{3,2},{4,5},{5,4},{6,7},{7,6},{8,9},{9,8},{10,11... | collective-permute-start | bytes 24584 | tf_op jit(solution)/shard_map/ppermute | solution.py:204

commit v2 on v0

v2 whole, which is shorter than its diff:
```python
import functools
import math

import jax
import jax.numpy as jnp
from jax import lax
from jax.experimental import pallas as pl
from jax.experimental.pallas import tpu as pltpu
from jax.sharding import PartitionSpec as P


coupling = 0.05
near_limit = 0.04

AXES = ("blk", "grp")
LANES = 128
ROWS = 16
CHUNK_TILES = 4
AMP_ROWS = 16
FEATURES = 64

PI_HIGH = 3.140625
PI_LOW = math.pi - PI_HIGH
SIN_POLY = (-0.16666656732559204, 0.008332998491823673, -0.00019805235206149518, 2.5970118713303236e-06)
COS_POLY = (-0.4999992549419403, 0.04166382923722267, -0.0013854617718607187, 2.316308928129729e-05)


def horner(coefficients, value):
    total = value * coefficients[-1] + coefficients[-2]
    for entry in coefficients[-3::-1]:
        total = total * value + entry
    return total


def green_terms(delta_x, delta_y, delta_z):
    square = delta_x * delta_x + delta_y * delta_y + delta_z * delta_z
    inverse = jnp.where(square < near_limit, 0.0, lax.rsqrt(square))
    radius = square * inverse
    turns = jnp.floor(radius * (0.5 / math.pi) + 0.5)
    angle = (radius * 0.5 - turns * PI_HIGH) - turns * PI_LOW
    angle_sq = angle * angle
    half_sine = angle + angle * (angle_sq * horner(SIN_POLY, angle_sq))
    half_cosine = 1.0 + angle_sq * horner(COS_POLY, angle_sq)
    twice = half_sine + half_sine
    inverse_sq = inverse * inverse
    cube = inverse_sq * inverse
    cosine = (1.0 - twice * half_sine) * cube
    sine = (twice * half_cosine) * cube
    near = square - 1.0
    sine_r = sine * radius
    cosine_r = cosine * radius
    near_re = cosine * near - sine_r
    near_im = sine * near + cosine_r
    mixed_re = cosine + sine_r
    mixed_im = sine - cosine_r
    return (
        near_re,
        near_im,
        (mixed_re + mixed_re - near_re) * inverse_sq,
        (mixed_im + mixed_im - near_im) * inverse_sq,
    )


def split(value):
    high = value.astype(jnp.bfloat16)
    return high, (value - high.astype(jnp.float32)).astype(jnp.bfloat16)


def dot_t(left, right):
    return lax.dot_general(left, right, (((1,), (1,)), ((), ())), preferred_element_type=jnp.float32)


def project_kernel(
    mode_hbm, moment_hbm, place_hbm, detune_hbm, width_hbm, polar_re_hbm, polar_im_hbm,
    amp_ref, mode_ref, moment_ref, place_ref, detune_ref, width_ref, polar_re_ref, polar_im_ref, mode_sem, sem,
):
    pieces = 2
    depth = mode_ref.shape[0] // pieces
    loads = [
        pltpu.make_async_copy(mode_hbm.at[pl.ds(i * depth, depth)], mode_ref.at[pl.ds(i * depth, depth)], mode_sem.at[i])
        for i in range(pieces)
    ]
    small = [
        pltpu.make_async_copy(source, target, sem.at[i])
        for i, (source, target) in enumerate(
            (
                (moment_hbm, moment_ref),
                (place_hbm, place_ref),
                (detune_hbm, detune_ref),
                (width_hbm, width_ref),
                (polar_re_hbm, polar_re_ref),
                (polar_im_hbm, polar_im_ref),
            )
        )
    ]
    small[0].start()
    for load in loads:
        load.start()
    for load in small[1:]:
        load.start()
    small[0].wait()
    plain, swapped = [], []
    for axis_c in range(3):
        plain.append(jnp.concatenate([moment_ref[0, axis_c], moment_ref[1, axis_c]], axis=0))
        swapped.append(
            jnp.concatenate(
                [
                    piece
                    for drive in range(2)
                    for piece in (-moment_ref[drive, axis_c, 1:2, :], moment_ref[drive, axis_c, 0:1, :])
                ],
                axis=0,
            )
        )
    left_high, left_low = split(jnp.concatenate(plain + swapped, axis=1))
    for load in loads:
        load.wait()
    mode_high, mode_low = split(mode_ref[...])
    both = jnp.dot(jnp.concatenate([left_high, left_low], axis=0), mode_high, preferred_element_type=jnp.float32)
    amp = both[0:4] + both[4:8] + jnp.dot(left_high, mode_low, preferred_element_type=jnp.float32)
    for tile in range(amp.shape[1] // LANES):
        amp_ref[4 * tile : 4 * tile + 4, :] = amp[:, tile * LANES : (tile + 1) * LANES]
    for load in small[1:]:
        load.wait()


def join_kernel(moment_ref, moment_other_ref, place_ref, place_other_ref, amp_ref, out_ref):
    for axis_c in range(3):
        for drive in range(2):
            row = 4 * axis_c + 2 * drive
            out_ref[row : row + 2, :] = jnp.concatenate(
                [moment_ref[drive, axis_c], moment_other_ref[drive, axis_c]], axis=1
            )
    out_ref[12:15, :] = jnp.concatenate([place_ref[...], place_other_ref[...]], axis=1)
    out_ref[15:16, :] = jnp.zeros((1, out_ref.shape[1]), jnp.float32)
    out_ref[ROWS:, :] = amp_ref[...]


def merge_kernel(*refs):
    out_ref = refs[-1]
    rows = refs[0].shape[0] - AMP_ROWS
    for place, ref in enumerate(refs[:-1]):
        out_ref[place * rows : (place + 1) * rows, :] = ref[:rows, :]
    out_ref[(len(refs) - 1) * rows :, :] = sum(ref[rows:, :] for ref in refs[:-1])


def total_kernel(*refs):
    start = refs[0].shape[0] - AMP_ROWS
    refs[-1][...] = sum(ref[start:, :] for ref in refs[:-1])


def prepare_kernel(
    mode_ref, place_ref, moment_ref, detune_ref, width_ref, polar_re_ref, polar_im_ref,
    high_ref, low_ref, column_ref, centre_ref, straight_ref, crossed_ref, base_ref,
):
    high_ref[...], low_ref[...] = split(jnp.transpose(mode_ref[...], (1, 0)))
    targets = place_ref.shape[1]
    for axis_c in range(3):
        row = place_ref[axis_c : axis_c + 1, :]
        column_ref[axis_c] = jnp.transpose(jnp.broadcast_to(row, (LANES, targets)), (1, 0))
        middle = jnp.sum(row, axis=1, keepdims=True) * (1.0 / targets)
        centre_ref[axis_c : axis_c + 1, :] = jnp.broadcast_to(middle, (1, LANES))
    detune, width = detune_ref[...], width_ref[...]
    denominator = detune * detune + width * width
    resp_re, resp_im = detune / denominator, width / denominator
    for tile in range(detune.shape[1] // LANES):
        lanes = slice(tile * LANES, (tile + 1) * LANES)
        for drive in range(2):
            row = 4 * tile + 2 * drive
            straight_ref[row : row + 2, :] = jnp.broadcast_to(resp_re[:, lanes], (2, LANES))
            crossed_ref[row : row + 1, :] = -resp_im[:, lanes]
            crossed_ref[row + 1 : row + 2, :] = resp_im[:, lanes]
    polar_re, polar_im = polar_re_ref[...], polar_im_ref[...]
    for axis_c in range(3):
        for drive in range(2):
            row = 4 * axis_c + 2 * drive
            moment_re = moment_ref[drive, axis_c, 0:1, :]
            moment_im = moment_ref[drive, axis_c, 1:2, :]
            base_ref[row : row + 1, :] = polar_re * moment_re - polar_im * moment_im
            base_ref[row + 1 : row + 2, :] = polar_re * moment_im + polar_im * moment_re


def accumulate_pairs(chips, centre_ref, target_ref, source_ref, out_ref, green_ref, feature_ref):
    targets = target_ref.shape[1]
    centre = [centre_ref[axis_c : axis_c + 1, 0:1] for axis_c in range(3)]

    def chunk(step, first):
        for tile in range(first, first + CHUNK_TILES):
            base = (step * CHUNK_TILES + tile - first) * ROWS
            if not isinstance(base, int):
                base = pl.multiple_of(base, ROWS)
            block = source_ref[pl.ds(base, ROWS), :]
            place = [block[12 + axis_c : 13 + axis_c, :] for axis_c in range(3)]
            local = [place[axis_c] - centre[axis_c] for axis_c in range(3)]
            moment = [block[4 * axis_c : 4 * axis_c + 4, :] for axis_c in range(3)]
            along = moment[0] * local[0] + moment[1] * local[1] + moment[2] * local[2]
            features = jnp.concatenate(
                [block[:12]]
                + [block[:12] * local[axis_c] for axis_c in range(3)]
                + [along * local[axis_c] for axis_c in range(3)]
                + [jnp.zeros_like(along)],
                axis=0,
            )
            high, (middle, low) = split3(features)
            feature_ref[tile, 0:FEATURES, :] = high
            feature_ref[tile, FEATURES : 2 * FEATURES, :] = middle
            feature_ref[tile, 2 * FEATURES :, :] = low
            for group in range(targets // 16):
                rows = slice(group * 16, group * 16 + 16)
                deltas = [
                    target_ref[axis_c, rows, :] - jnp.broadcast_to(place[axis_c], (16, LANES)) for axis_c in range(3)
                ]
                for part, entry in enumerate(green_terms(*deltas)):
                    start = part * targets + group * 16
                    high, rest = split3(entry, part >= 2)
                    green_ref[tile, start : start + 16, :] = high
                    green_ref[tile, 4 * targets + start : 4 * targets + start + 16, :] = rest[0]
                    if part >= 2:
                        green_ref[tile, 6 * targets + start : 6 * targets + start + 16, :] = rest[1]
        out_ref[...] += dot_t(
            jnp.concatenate([green_ref[tile] for tile in range(first, first + CHUNK_TILES)], axis=1),
            jnp.concatenate([feature_ref[tile] for tile in range(first, first + CHUNK_TILES)], axis=1),
        )

    steps = chips // CHUNK_TILES
    if steps == 1:
        chunk(0, 0)
    else:
        pl.loop(0, steps)(lambda step: chunk(step, 0))


def split3(value, three=True):
    high = value.astype(jnp.bfloat16)
    rest = value - high.astype(jnp.float32)
    middle = rest.astype(jnp.bfloat16)
    if not three:
        return high, (middle,)
    return high, (middle, (rest - middle.astype(jnp.float32)).astype(jnp.bfloat16))


def first_pair_kernel(chips, centre_ref, target_ref, source_ref, out_ref, green_ref, feature_ref):
    out_ref[...] = jnp.zeros_like(out_ref)
    accumulate_pairs(chips, centre_ref, target_ref, source_ref, out_ref, green_ref, feature_ref)


def next_pair_kernel(chips, centre_ref, target_ref, source_ref, before_ref, out_ref, green_ref, feature_ref):
    out_ref[...] = before_ref[...]
    accumulate_pairs(chips, centre_ref, target_ref, source_ref, out_ref, green_ref, feature_ref)


def complex_rows(real, imag):
    out = []
    for drive in range(2):
        out.append(real[2 * drive : 2 * drive + 1] - imag[2 * drive + 1 : 2 * drive + 2])
        out.append(real[2 * drive + 1 : 2 * drive + 2] + imag[2 * drive : 2 * drive + 1])
    return jnp.concatenate(out, axis=0)


def last_pair_kernel(
    chips, centre_ref, target_ref, source_ref, first_ref, place_ref, base_ref, out_ref, sum_ref, green_ref, feature_ref
):
    sum_ref[...] = first_ref[...]
    accumulate_pairs(chips, centre_ref, target_ref, source_ref, sum_ref, green_ref, feature_ref)
    targets = place_ref.shape[1]
    raw = sum_ref[0 : 4 * targets, :] + sum_ref[4 * targets : 8 * targets, :]
    raw = jnp.concatenate([raw[: 2 * targets], raw[2 * targets :] + sum_ref[8 * targets :, :]], axis=0)
    raw = jnp.transpose(raw, (1, 0))
    raw = raw[0:FEATURES] + raw[FEATURES : 2 * FEATURES] + raw[2 * FEATURES :]
    near_re, near_im, far_re, far_im = [raw[:, part * targets : (part + 1) * targets] for part in range(4)]
    local = [place_ref[axis_c : axis_c + 1, :] - centre_ref[axis_c : axis_c + 1, 0:1] for axis_c in range(3)]

    def rows_of(table, group, axis_c):
        return table[12 * group + 4 * axis_c : 12 * group + 4 * axis_c + 4]

    def outer(table, axis_c):
        straight = sum(local[j] * rows_of(table, 0, j) for j in range(3))
        dotted = sum(rows_of(table, 1 + j, j) for j in range(3))
        crossed = sum(local[j] * rows_of(table, 1 + axis_c, j) for j in range(3))
        return local[axis_c] * (straight - dotted) - crossed + rows_of(table, 4, axis_c)

    for axis_c in range(3):
        pair = complex_rows(
            rows_of(near_re, 0, axis_c) + outer(far_re, axis_c), rows_of(near_im, 0, axis_c) + outer(far_im, axis_c)
        )
        out_ref[4 * axis_c : 4 * axis_c + 4, :] = base_ref[4 * axis_c : 4 * axis_c + 4, :] - coupling * pair


def finish_kernel(mine_ref, other_ref, high_ref, low_ref, straight_ref, crossed_ref, rest_ref, out_ref):
    targets = rest_ref.shape[1]
    amp = mine_ref[...] + other_ref[...]
    rows = amp.shape[0]
    odd = (lax.broadcasted_iota(jnp.int32, amp.shape, 0) & 1) == 1
    partner = jnp.where(odd, pltpu.roll(amp, 1, 0), pltpu.roll(amp, rows - 1, 0))
    weighted = straight_ref[...] * amp + crossed_ref[...] * partner
    weighted = jnp.concatenate([weighted[4 * tile : 4 * tile + 4] for tile in range(rows // 4)], axis=1)
    weight_high, weight_low = split(weighted)
    both = jnp.dot(
        jnp.concatenate([weight_high, weight_low], axis=0), high_ref[...], preferred_element_type=jnp.float32
    )
    modal = both[0:4] + both[4:8] + jnp.dot(weight_high, low_ref[...], preferred_element_type=jnp.float32)
    half = 3 * targets
    for axis_c in range(3):
        mode_re = modal[:, axis_c * targets : (axis_c + 1) * targets]
        mode_im = modal[:, half + axis_c * targets : half + (axis_c + 1) * targets]
        result = rest_ref[4 * axis_c : 4 * axis_c + 4, :] - complex_rows(mode_re, mode_im)
        out_ref[0, axis_c] = result[0:2]
        out_ref[1, axis_c] = result[2:4]


def kernel_call(body, outs, operands, scratch=(), flops=100_000, loads=False):
    single = not isinstance(outs, tuple)
    vmem = pl.BlockSpec(memory_space=pltpu.VMEM)
    source = pl.BlockSpec(memory_space=pltpu.HBM) if loads else vmem
    return pl.pallas_call(
        body,
        out_shape=outs,
        in_specs=[source] * len(operands),
        out_specs=vmem if single else (vmem,) * len(outs),
        scratch_shapes=list(scratch),
        cost_estimate=pl.CostEstimate(flops=flops, bytes_accessed=100_000, transcendentals=0),
        compiler_params=pltpu.CompilerParams(vmem_limit_bytes=12 * 1024 * 1024),
    )(*operands)


def on_device(devices, positions, moments, inv_polar_re, inv_polar_im, mode_field, mode_detune, mode_width):
    targets = positions.shape[1]
    modes = mode_field.shape[3]

    def shape(*dims, dtype=jnp.float32):
        return jax.ShapeDtypeStruct(dims, dtype)

    def exchange(value, distance):
        return lax.ppermute(value, AXES, [(i, i ^ distance) for i in range(devices)])

    def like(value):
        return shape(*value.shape)

    moments = jnp.transpose(moments, (0, 2, 1, 3))
    mode_rows = mode_field.reshape(6 * targets, modes)
    moments_other = exchange(moments, 1)
    positions_other = exchange(positions, 1)
    inputs = tuple(pltpu.with_memory_space_constraint(value, pltpu.HBM) for value in (
        mode_rows,
        moments,
        positions,
        mode_detune[None],
        mode_width[None],
        inv_polar_re[None],
        inv_polar_im[None],
    ))
    amp, mode_rows, moments, positions, detune, width, polar_re, polar_im = kernel_call(
        project_kernel,
        (shape(AMP_ROWS, LANES),) + tuple(like(value) for value in inputs),
        inputs,
        [pltpu.SemaphoreType.DMA((2,)), pltpu.SemaphoreType.DMA((6,))],
        flops=5_000_000,
        loads=True,
    )
    message = kernel_call(
        join_kernel, shape(ROWS + AMP_ROWS, LANES), (moments, moments_other, positions, positions_other, amp)
    )
    mode_high, mode_low, columns, centre, straight, crossed, base = kernel_call(
        prepare_kernel,
        (
            shape(modes, 6 * targets, dtype=jnp.bfloat16),
            shape(modes, 6 * targets, dtype=jnp.bfloat16),
            shape(3, targets, LANES),
            shape(8, LANES),
            shape(AMP_ROWS, LANES),
            shape(AMP_ROWS, LANES),
            shape(12, targets),
        ),
        (mode_rows, positions, moments, detune, width, polar_re, polar_im),
        flops=5_000_000,
    )
    distance = devices // 2
    while distance > 4:
        steps = (distance ^ 1, (3 * distance // 2) ^ 1, distance // 2) if distance > 8 else (distance ^ 1,)
        arrived = [exchange(message, step) for step in steps]
        rows = message.shape[0] - AMP_ROWS
        message = kernel_call(merge_kernel, shape((1 + len(steps)) * rows + AMP_ROWS, LANES), (message, *arrived))
        distance //= 4 if len(steps) == 3 else 2
    chips = (message.shape[0] - AMP_ROWS) // ROWS
    diagonal = exchange(message, 6)
    side = exchange(message, 4 ^ 1)
    near = exchange(message, 2 ^ 1)
    sums = shape(10 * targets, 3 * FEATURES)
    scratch = [
        pltpu.VMEM((CHUNK_TILES, 10 * targets, LANES), jnp.bfloat16),
        pltpu.VMEM((CHUNK_TILES, 3 * FEATURES, LANES), jnp.bfloat16),
    ]

    def pair(kernel, source, *more, out=sums, extra=()):
        return kernel_call(
            functools.partial(kernel, chips),
            out,
            (centre, columns, source) + more,
            list(extra) + scratch,
            flops=20_000_000,
        )

    partial_sums = pair(first_pair_kernel, message)
    partial_sums = pair(next_pair_kernel, diagonal, partial_sums)
    mine = kernel_call(total_kernel, shape(AMP_ROWS, LANES), (message, diagonal, side, near))
    other = exchange(mine, 1)
    partial_sums = pair(next_pair_kernel, side, partial_sums)
    rest = pair(
        last_pair_kernel,
        near,
        partial_sums,
        positions,
        base,
        out=shape(12, targets),
        extra=(pltpu.VMEM(sums.shape, jnp.float32),),
    )
    out = kernel_call(
        finish_kernel, shape(2, 3, 2, targets), (mine, other, mode_high, mode_low, straight, crossed, rest)
    )
    return jnp.transpose(out, (0, 2, 1, 3))


def solution(mesh):
    placed = (
        P(None, AXES),
        P(None, None, None, AXES),
        P(AXES),
        P(AXES),
        P(None, None, AXES, None),
        P(),
        P(),
    )
    return jax.shard_map(
        functools.partial(on_device, mesh.size),
        mesh=mesh,
        in_specs=placed,
        out_specs=P(None, None, None, AXES),
        check_vma=False,
    )
```

time: 127 us -> 22.2 us (0.17)
  blocking collectives: 114 us -> 0 us
  starting transfers between devices: 0 us -> 9.41 us
  waiting for transfers between devices: 0 us -> 6.6 us
  Pallas kernels: 0 us -> 5.95 us
  other arithmetic: 5.14 us -> 0 us
  local copies, waits for them, and re-layouts: 4.42 us -> 0 us
  matrix products: 2.95 us -> 0 us
    all_gather x4 -> x0, blocking collectives: 71.8 us -> none  [the longest x1 30.6 us: on_device(): places = lax.all_gather(group_pos, 'blk', axis=1, tiled=True)]
    psum x1 -> x0, blocking collectives: 42.1 us -> none  [on_device(): amp_re, amp_im = lax.psum((amp_re, amp_im), ('blk', 'grp'))]
    ppermute x0 -> x9, starting transfers between devices: none -> 9.41 us  [exchange(): lax.ppermute(value, AXES, [(i, i ^ distance) for i in range(devices)])]
    ppermute x0 -> x9, waiting for transfers between devices: none -> 6.6 us  [exchange(): lax.ppermute(value, AXES, [(i, i ^ distance) for i in range(devices)])]
    pallas_call x0 -> x10, Pallas kernels: none -> 5.95 us  [kernel_call(): pl.pallas_call(body, out_shape=outs, in_specs=[source] * len(operands), o...]
    reduce_sum x1 -> x0, other arithmetic: 5.11 us -> none  [pair_field(): jnp.sum(entry_tile, axis=axis_sum)]
    dot_general x8 -> x0, matrix products: 2.95 us -> none  [the longest x4 1.66 us: spread(): lax.dot_general(weights, rows, (((0,), (1,)), ((), ())), precision=lax.Pr...]
    unnamed x15 -> x0, local copies, waits for them, and re-layouts: 2.18 us -> none
  transfers between devices with their start and end apart: 0 -> 9, of which waited for: 0 -> 4; matrix products, arithmetic and copies ran while one was open for 0% -> 0% of each run, Pallas kernels for 0% -> 22%
where the time goes in v2:
time: 22.2 us; the launch traced here: 22 us
  starting transfers between devices  9.41 us (42%)
  waiting for transfers between devices  6.6 us (30%)
  Pallas kernels  5.95 us (27%)
    ppermute x9, starting transfers between devices, exchange(): lax.ppermute(value, AXES, [(i, i ^ distance) for i in range(devices)])  9.41 us
    ppermute x9, waiting for transfers between devices, exchange(): lax.ppermute(value, AXES, [(i, i ^ distance) for i in range(devices)])  6.6 us
    pallas_call x10, Pallas kernels, kernel_call(): pl.pallas_call(body, out_shape=outs, in_specs=[source] * len(operands), o...  5.95 us
  transfers between devices with their start and end apart: 9, of which 4 were waited for; matrix products, arithmetic and copies ran while one was open for 0% of the time, Pallas kernels for 22%

profile of v2, /device:TPU:0, one launch (start us, length us, event | category | flops | bytes accessed | tf_op | source)
XLA Modules:
  0.0 22.0 jit_solution(1892418928190274488)
XLA Ops:
  0.0 0.5 %collective-permute-start = (f32[2,3,2,64]{3,2,1,0:T(2,128)}, f32[2,3,2,64]{3,2,1,0:T(2,128)S(1)}, u32[]{:S(2)}, u32[]{:S(2)}) collective-permute-start(f32[2,3,2,64]{3,2,1,0:T(2,128)} %bitcast.8), channel_id=1, source_target_pairs={{0,1},{1,0},{2,3},{3,2},{4,5},{5,4},{6,7},{7,6},{8,9},{9,8},{10,11... | collective-permute-start | bytes 9224 | tf_op jit(solution)/shard_map/ppermute | solution.py:333
  0.5 0.0 collective-permute-start.1
  0.5 1.5 %shard_map.73 = (f32[16,128]{1,0:T(8,128)S(1)}, f32[384,512]{1,0:T(8,128)S(1)}, f32[2,3,2,64]{3,2,1,0:T(2,128)S(1)}, f32[3,64]{1,0:T(4,128)S(1)}, f32[1,512]{1,0...) custom-call(f32[384,512]{1,0:T(8,128)} %bitcast.7, f32[2,3,2,64]{3,2,1,0:T(2,128)} %bitcast.9, ...), custom_call_target="tpu_custom_call" | custom-call | flops 5000000 | bytes 100000 | tf_op jit(solution)/shard_map/pallas_call | solution.py:314
  2.0 0.0 collective-permute-done.1.place_other_ref
  2.0 0.0 collective-permute-done.moment_other_ref
  2.0 0.1 shard_map.74.refs_0_
  2.1 3.7 %collective-permute-start.2 = (f32[32,128]{1,0:T(8,128)S(1)}, f32[32,128]{1,0:T(8,128)S(1)}, u32[]{:S(2)}, u32[]{:S(2)}) collective-permute-start(f32[32,128]{1,0:T(8,128)S(1)} %shard_map.74.refs_0_), channel_id=1, source_target_pairs={{0,17},{1,16},{2,19},{3,18},{4,21},{5,20},{6,23},{7,22},{8,25},{9,... | collective-permute-start | bytes 49160 | tf_op jit(solution)/shard_map/ppermute | solution.py:333
  5.8 1.5 %collective-permute-start.3 = (f32[32,128]{1,0:T(8,128)S(1)}, f32[32,128]{1,0:T(8,128)S(1)}, u32[]{:S(2)}, u32[]{:S(2)}) collective-permute-start(f32[32,128]{1,0:T(8,128)S(1)} %shard_map.74.refs_0_), channel_id=1, source_target_pairs={{0,25},{1,24},{2,27},{3,26},{4,29},{5,28},{6,31},{7,30},{8,17},{9,... | collective-permute-start | bytes 49160 | tf_op jit(solution)/shard_map/ppermute | solution.py:333
  7.3 0.1 collective-permute-start.4
  7.4 0.0 collective-permute-done.2.refs_1_
  7.4 3.5 %collective-permute-done.3.refs_2_ = f32[32,128]{1,0:T(8,128)S(1)} collective-permute-done((f32[32,128]{1,0:T(8,128)S(1)}, f32[32,128]{1,0:T(8,128)S(1)}, u32[]{:S(2)}, u32[]{:S(2)}) %collective-permute-start.3) | collective-permute-done | bytes 16416 | tf_op jit(solution)/shard_map/ppermute | solution.py:333
  10.8 0.2 collective-permute-done.4.refs_3_
  11.0 2.5 %collective-permute-start.5 = (f32[80,128]{1,0:T(8,128)S(1)}, f32[80,128]{1,0:T(8,128)S(1)}, u32[]{:S(2)}, u32[]{:S(2)}) collective-permute-start(f32[80,128]{1,0:T(8,128)S(1)} %shard_map.75.refs_0_.source_ref), channel_id=1, source_target_pairs={{0,6},{1,7},{2,4},{3,5},{4,2},{5,3},{6,0},{7,1},{8,14},{9,15},{10,... | collective-permute-start | bytes 122888 | tf_op jit(solution)/shard_map/ppermute | solution.py:333
  13.5 0.1 collective-permute-start.6
  13.7 0.6 %collective-permute-start.7 = (f32[80,128]{1,0:T(8,128)S(1)}, f32[80,128]{1,0:T(8,128)S(1)}, u32[]{:S(2)}, u32[]{:S(2)}) collective-permute-start(f32[80,128]{1,0:T(8,128)S(1)} %shard_map.75.refs_0_.source_ref), channel_id=1, source_target_pairs={{0,3},{1,2},{2,1},{3,0},{4,7},{5,6},{6,5},{7,4},{8,11},{9,10},{10,... | collective-permute-start | bytes 122888 | tf_op jit(solution)/shard_map/ppermute | solution.py:333
  14.3 1.7 %collective-permute-done.5.refs_1_.source_ref = f32[80,128]{1,0:T(8,128)S(1)} collective-permute-done((f32[80,128]{1,0:T(8,128)S(1)}, f32[80,128]{1,0:T(8,128)S(1)}, u32[]{:S(2)}, u32[]{:S(2)}) %collective-permute-start.5) | collective-permute-done | bytes 40992 | tf_op jit(solution)/shard_map/ppermute | solution.py:333
  16.0 1.3 %collective-permute-done.6.refs_2_.source_ref = f32[80,128]{1,0:T(8,128)S(1)} collective-permute-done((f32[80,128]{1,0:T(8,128)S(1)}, f32[80,128]{1,0:T(8,128)S(1)}, u32[]{:S(2)}, u32[]{:S(2)}) %collective-permute-start.6) | collective-permute-done | bytes 40992 | tf_op jit(solution)/shard_map/ppermute | solution.py:333
  17.2 0.0 collective-permute-done.7.refs_3_.source_ref
  17.2 0.4 %collective-permute-start.8 = (f32[16,128]{1,0:T(8,128)S(1)}, f32[16,128]{1,0:T(8,128)S(1)}, u32[]{:S(2)}, u32[]{:S(2)}) collective-permute-start(f32[16,128]{1,0:T(8,128)S(1)} %shard_map.76.mine_ref), channel_id=1, source_target_pairs={{0,1},{1,0},{2,3},{3,2},{4,5},{5,4},{6,7},{7,6},{8,9},{9,8},{10,11... | collective-permute-start | bytes 24584 | tf_op jit(solution)/shard_map/ppermute | solution.py:333
  17.6 0.3 %shard_map.77 = (bf16[512,384]{1,0:T(8,128)(2,1)S(1)}, bf16[512,384]{1,0:T(8,128)(2,1)S(1)}, f32[3,64,128]{2,1,0:T(8,128)S(1)}, f32[8,128]{1,0:T(8,128)S(1)}, f3...) custom-call(f32[384,512]{1,0:T(8,128)S(1)} %get-tuple-element.23.mode_ref, ...), custom_call_target="tpu_custom_call" | custom-call | flops 5000000 | bytes 100000 | tf_op jit(solution)/shard_map/pallas_call | solution.py:314
  18.0 0.7 %shard_map.78.before_ref = f32[640,192]{1,0:T(8,128)S(1)} custom-call(f32[8,128]{1,0:T(8,128)S(1)} %get-tuple-element.32.centre_ref, f32[3,64,128]{2,1,0:T(8,128)S(1)} %get-tuple-element.33.target_ref, f32[80,128]{1,0:T(8,128)S(1)} %shard_map.75.refs_0_.source_ref), custom_call_target="tpu_custom_call" | custom-call | flops 20000000 | bytes 100000 | tf_op jit(solution)/shard_map/pallas_call | solution.py:314
  18.7 0.7 %shard_map.79.before_ref = f32[640,192]{1,0:T(8,128)S(1)} custom-call(f32[8,128]{1,0:T(8,128)S(1)} %get-tuple-element.32.centre_ref, f32[3,64,128]{2,1,0:T(8,128)S(1)} %get-tuple-element.33.target_ref, f32[80,128]{1,0:T(8,128)S(1)} %collective-permute-done.5.refs_1_.source_ref, f32[640,192]{1,0:T(8,128)S(1)} %shard_map.78.before_ref), custom_call_target="tpu_custom_call" | custom-call | flops 20000000 | bytes 100000 | tf_op jit(solution)/shard_map/pallas_call | solution.py:314
  19.4 0.7 %shard_map.80.first_ref = f32[640,192]{1,0:T(8,128)S(1)} custom-call(f32[8,128]{1,0:T(8,128)S(1)} %get-tuple-element.32.centre_ref, f32[3,64,128]{2,1,0:T(8,128)S(1)} %get-tuple-element.33.target_ref, f32[80,128]{1,0:T(8,128)S(1)} %collective-permute-done.6.refs_2_.source_ref, f32[640,192]{1,0:T(8,128)S(1)} %shard_map.79.before_ref), custom_call_target="tpu_custom_call" | custom-call | flops 20000000 | bytes 100000 | tf_op jit(solution)/shard_map/pallas_call | solution.py:314
  20.0 1.0 %shard_map.81.rest_ref = f32[12,64]{1,0:T(8,128)S(1)} custom-call(f32[8,128]{1,0:T(8,128)S(1)} %get-tuple-element.32.centre_ref, f32[3,64,128]{2,1,0:T(8,128)S(1)} %get-tuple-element.33.target_ref, f32[80,128]{1,0:T(8,128)S(1)} %collective-permute-done.7.refs_3_.source_ref, f32[640,192]{1,0:T(8,128)S(1)} %shard_map.80.first_ref, ...), custom_call_target="tpu_custom_call" | custom-call | flops 20000000 | bytes 100000 | tf_op jit(solution)/shard_map/pallas_call | solution.py:314
  21.0 0.0 collective-permute-done.8.other_ref
  21.1 1.0 %shard_map.82 = f32[2,3,2,64]{3,2,1,0:T(2,128)} custom-call(f32[16,128]{1,0:T(8,128)S(1)} %shard_map.76.mine_ref, f32[16,128]{1,0:T(8,128)S(1)} %collective-permute-done.8.other_ref, bf16[512,384]{1,0:T(8,128)(2,1)S(1)} %get-tuple-element.28.high_ref, bf16[512,384]{1,0:T(8,128)(2,1)S(1)} %get-tuple-element.29.low_ref, ...), custom_call_target="tpu_custom_call" | custom-call | flops 100000 | bytes 100000 | tf_op jit(solution)/shard_map/pallas_call | solution.py:314
  (2 shorter events, 0.0 us)
Async XLA Ops:
  0.0 2.0 %collective-permute-start = (f32[2,3,2,64]{3,2,1,0:T(2,128)}, f32[2,3,2,64]{3,2,1,0:T(2,128)S(1)}, u32[]{:S(2)}, u32[]{:S(2)}) collective-permute-start(f32[2,3,2,64]{3,2,1,0:T(2,128)} %bitcast.8), channel_id=1, source_target_pairs={{0,1},{1,0},{2,3},{3,2},{4,5},{5,4},{6,7},{7,6},{8,9},{9,8},{10,11... | collective-permute-start | bytes 9224 | tf_op jit(solution)/shard_map/ppermute | solution.py:333
  0.5 1.5 %collective-permute-start.1 = (f32[3,64]{1,0:T(4,128)}, f32[3,64]{1,0:T(4,128)S(1)}, u32[]{:S(2)}, u32[]{:S(2)}) collective-permute-start(f32[3,64]{1,0:T(4,128)} %place_hbm.1), channel_id=1, source_target_pairs={{0,1},{1,0},{2,3},{3,2},{4,5},{5,4},{6,7},{7,6},{8,9},{9,8},{10,11... | collective-permute-start | bytes 2312 | tf_op jit(solution)/shard_map/ppermute | solution.py:333
  2.1 5.3 %collective-permute-start.2 = (f32[32,128]{1,0:T(8,128)S(1)}, f32[32,128]{1,0:T(8,128)S(1)}, u32[]{:S(2)}, u32[]{:S(2)}) collective-permute-start(f32[32,128]{1,0:T(8,128)S(1)} %shard_map.74.refs_0_), channel_id=1, source_target_pairs={{0,17},{1,16},{2,19},{3,18},{4,21},{5,20},{6,23},{7,22},{8,25},{9,... | collective-permute-start | bytes 49160 | tf_op jit(solution)/shard_map/ppermute | solution.py:333
  5.8 5.0 %collective-permute-start.3 = (f32[32,128]{1,0:T(8,128)S(1)}, f32[32,128]{1,0:T(8,128)S(1)}, u32[]{:S(2)}, u32[]{:S(2)}) collective-permute-start(f32[32,128]{1,0:T(8,128)S(1)} %shard_map.74.refs_0_), channel_id=1, source_target_pairs={{0,25},{1,24},{2,27},{3,26},{4,29},{5,28},{6,31},{7,30},{8,17},{9,... | collective-permute-start | bytes 49160 | tf_op jit(solution)/shard_map/ppermute | solution.py:333
  7.3 3.8 %collective-permute-start.4 = (f32[32,128]{1,0:T(8,128)S(1)}, f32[32,128]{1,0:T(8,128)S(1)}, u32[]{:S(2)}, u32[]{:S(2)}) collective-permute-start(f32[32,128]{1,0:T(8,128)S(1)} %shard_map.74.refs_0_), channel_id=1, source_target_pairs={{0,8},{1,9},{2,10},{3,11},{4,12},{5,13},{6,14},{7,15},{8,0},{9,1},... | collective-permute-start | bytes 49160 | tf_op jit(solution)/shard_map/ppermute | solution.py:333
  11.0 5.0 %collective-permute-start.5 = (f32[80,128]{1,0:T(8,128)S(1)}, f32[80,128]{1,0:T(8,128)S(1)}, u32[]{:S(2)}, u32[]{:S(2)}) collective-permute-start(f32[80,128]{1,0:T(8,128)S(1)} %shard_map.75.refs_0_.source_ref), channel_id=1, source_target_pairs={{0,6},{1,7},{2,4},{3,5},{4,2},{5,3},{6,0},{7,1},{8,14},{9,15},{10,... | collective-permute-start | bytes 122888 | tf_op jit(solution)/shard_map/ppermute | solution.py:333
  13.5 3.7 %collective-permute-start.6 = (f32[80,128]{1,0:T(8,128)S(1)}, f32[80,128]{1,0:T(8,128)S(1)}, u32[]{:S(2)}, u32[]{:S(2)}) collective-permute-start(f32[80,128]{1,0:T(8,128)S(1)} %shard_map.75.refs_0_.source_ref), channel_id=1, source_target_pairs={{0,5},{1,4},{2,7},{3,6},{4,1},{5,0},{6,3},{7,2},{8,13},{9,12},{10,... | collective-permute-start | bytes 122888 | tf_op jit(solution)/shard_map/ppermute | solution.py:333
  13.7 3.6 %collective-permute-start.7 = (f32[80,128]{1,0:T(8,128)S(1)}, f32[80,128]{1,0:T(8,128)S(1)}, u32[]{:S(2)}, u32[]{:S(2)}) collective-permute-start(f32[80,128]{1,0:T(8,128)S(1)} %shard_map.75.refs_0_.source_ref), channel_id=1, source_target_pairs={{0,3},{1,2},{2,1},{3,0},{4,7},{5,6},{6,5},{7,4},{8,11},{9,10},{10,... | collective-permute-start | bytes 122888 | tf_op jit(solution)/shard_map/ppermute | solution.py:333
  17.2 3.8 %collective-permute-start.8 = (f32[16,128]{1,0:T(8,128)S(1)}, f32[16,128]{1,0:T(8,128)S(1)}, u32[]{:S(2)}, u32[]{:S(2)}) collective-permute-start(f32[16,128]{1,0:T(8,128)S(1)} %shard_map.76.mine_ref), channel_id=1, source_target_pairs={{0,1},{1,0},{2,3},{3,2},{4,5},{5,4},{6,7},{7,6},{8,9},{9,8},{10,11... | collective-permute-start | bytes 24584 | tf_op jit(solution)/shard_map/ppermute | solution.py:333

commit v3 on v2

--- a/solution.py
+++ b/solution.py
@@ -16,8 +16,10 @@
 LANES = 128
 ROWS = 16
 CHUNK_TILES = 4
+PIECES = 3
 AMP_ROWS = 16
 FEATURES = 64
+GROUP = 32
 
 PI_HIGH = 3.140625
 PI_LOW = math.pi - PI_HIGH
@@ -70,28 +72,16 @@
     return lax.dot_general(left, right, (((1,), (1,)), ((), ())), preferred_element_type=jnp.float32)
 
 
-def project_kernel(
-    mode_hbm, moment_hbm, place_hbm, detune_hbm, width_hbm, polar_re_hbm, polar_im_hbm,
-    amp_ref, mode_ref, moment_ref, place_ref, detune_ref, width_ref, polar_re_ref, polar_im_ref, mode_sem, sem,
-):
-    pieces = 2
+def project_kernel(mode_hbm, moment_hbm, place_hbm, amp_ref, mode_ref, moment_ref, place_ref, mode_sem, sem):
+    pieces = PIECES
     depth = mode_ref.shape[0] // pieces
     loads = [
         pltpu.make_async_copy(mode_hbm.at[pl.ds(i * depth, depth)], mode_ref.at[pl.ds(i * depth, depth)], mode_sem.at[i])
         for i in range(pieces)
     ]
     small = [
-        pltpu.make_async_copy(source, target, sem.at[i])
-        for i, (source, target) in enumerate(
-            (
-                (moment_hbm, moment_ref),
-                (place_hbm, place_ref),
-                (detune_hbm, detune_ref),
-                (width_hbm, width_ref),
-                (polar_re_hbm, polar_re_ref),
-                (polar_im_hbm, polar_im_ref),
-            )
-        )
+        pltpu.make_async_copy(moment_hbm, moment_ref, sem.at[0]),
+        pltpu.make_async_copy(place_hbm, place_ref, sem.at[1]),
     ]
     small[0].start()
     for load in loads:
@@ -113,11 +103,15 @@
             )
         )
     left_high, left_low = split(jnp.concatenate(plain + swapped, axis=1))
-    for load in loads:
+    both_left = jnp.concatenate([left_high, left_low], axis=0)
+    both, rest = 0.0, 0.0
+    for i, load in enumerate(loads):
         load.wait()
-    mode_high, mode_low = split(mode_ref[...])
-    both = jnp.dot(jnp.concatenate([left_high, left_low], axis=0), mode_high, preferred_element_type=jnp.float32)
-    amp = both[0:4] + both[4:8] + jnp.dot(left_high, mode_low, preferred_element_type=jnp.float32)
+        piece = slice(i * depth, (i + 1) * depth)
+        mode_high, mode_low = split(mode_ref[piece, :])
+        both += jnp.dot(both_left[:, piece], mode_high, preferred_element_type=jnp.float32)
+        rest += jnp.dot(left_high[:, piece], mode_low, preferred_element_type=jnp.float32)
+    amp = both[0:4] + both[4:8] + rest
     for tile in range(amp.shape[1] // LANES):
         amp_ref[4 * tile : 4 * tile + 4, :] = amp[:, tile * LANES : (tile + 1) * LANES]
     for load in small[1:]:
@@ -150,9 +144,23 @@
 
 
 def prepare_kernel(
-    mode_ref, place_ref, moment_ref, detune_ref, width_ref, polar_re_ref, polar_im_ref,
+    mode_ref, place_ref, moment_ref, detune_hbm, width_hbm, polar_re_hbm, polar_im_hbm,
     high_ref, low_ref, column_ref, centre_ref, straight_ref, crossed_ref, base_ref,
+    detune_ref, width_ref, polar_re_ref, polar_im_ref, sem,
 ):
+    loads = [
+        pltpu.make_async_copy(source, target, sem.at[i])
+        for i, (source, target) in enumerate(
+            (
+                (detune_hbm, detune_ref),
+                (width_hbm, width_ref),
+                (polar_re_hbm, polar_re_ref),
+                (polar_im_hbm, polar_im_ref),
+            )
+        )
+    ]
+    for load in loads:
+        load.start()
     high_ref[...], low_ref[...] = split(jnp.transpose(mode_ref[...], (1, 0)))
     targets = place_ref.shape[1]
     for axis_c in range(3):
@@ -160,6 +168,8 @@
         column_ref[axis_c] = jnp.transpose(jnp.broadcast_to(row, (LANES, targets)), (1, 0))
         middle = jnp.sum(row, axis=1, keepdims=True) * (1.0 / targets)
         centre_ref[axis_c : axis_c + 1, :] = jnp.broadcast_to(middle, (1, LANES))
+    for load in loads:
+        load.wait()
     detune, width = detune_ref[...], width_ref[...]
     denominator = detune * detune + width * width
     resp_re, resp_im = detune / denominator, width / denominator
@@ -180,17 +190,22 @@
             base_ref[row + 1 : row + 2, :] = polar_re * moment_im + polar_im * moment_re
 
 
-def accumulate_pairs(chips, centre_ref, target_ref, source_ref, out_ref, green_ref, feature_ref):
-    targets = target_ref.shape[1]
+def accumulate_pairs(chips, centre_ref, target_ref, source_refs, before_ref, out_ref, green_ref, feature_ref):
+    groups = target_ref.shape[1] // GROUP
+    depth = 10 * GROUP
     centre = [centre_ref[axis_c : axis_c + 1, 0:1] for axis_c in range(3)]
 
-    def chunk(step, first):
-        for tile in range(first, first + CHUNK_TILES):
-            base = (step * CHUNK_TILES + tile - first) * ROWS
+    tiles = CHUNK_TILES * len(source_refs)
+
+    def chunk(step, before_ref):
+        places = []
+        for tile in range(tiles):
+            base = (step * CHUNK_TILES + tile % CHUNK_TILES) * ROWS
             if not isinstance(base, int):
                 base = pl.multiple_of(base, ROWS)
-            block = source_ref[pl.ds(base, ROWS), :]
+            block = source_refs[tile // CHUNK_TILES][pl.ds(base, ROWS), :]
             place = [block[12 + axis_c : 13 + axis_c, :] for axis_c in range(3)]
+            places.append([jnp.broadcast_to(row, (16, LANES)) for row in place])
             local = [place[axis_c] - centre[axis_c] for axis_c in range(3)]
             moment = [block[4 * axis_c : 4 * axis_c + 4, :] for axis_c in range(3)]
             along = moment[0] * local[0] + moment[1] * local[1] + moment[2] * local[2]
@@ -205,28 +220,26 @@
             feature_ref[tile, 0:FEATURES, :] = high
             feature_ref[tile, FEATURES : 2 * FEATURES, :] = middle
             feature_ref[tile, 2 * FEATURES :, :] = low
-            for group in range(targets // 16):
-                rows = slice(group * 16, group * 16 + 16)
-                deltas = [
-                    target_ref[axis_c, rows, :] - jnp.broadcast_to(place[axis_c], (16, LANES)) for axis_c in range(3)
-                ]
-                for part, entry in enumerate(green_terms(*deltas)):
-                    start = part * targets + group * 16
-                    high, rest = split3(entry, part >= 2)
-                    green_ref[tile, start : start + 16, :] = high
-                    green_ref[tile, 4 * targets + start : 4 * targets + start + 16, :] = rest[0]
-                    if part >= 2:
-                        green_ref[tile, 6 * targets + start : 6 * targets + start + 16, :] = rest[1]
-        out_ref[...] += dot_t(
-            jnp.concatenate([green_ref[tile] for tile in range(first, first + CHUNK_TILES)], axis=1),
-            jnp.concatenate([feature_ref[tile] for tile in range(first, first + CHUNK_TILES)], axis=1),
-        )
-
-    steps = chips // CHUNK_TILES
-    if steps == 1:
-        chunk(0, 0)
-    else:
-        pl.loop(0, steps)(lambda step: chunk(step, 0))
+        for group in range(groups):
+            for tile in range(tiles):
+                for piece in range(GROUP // 16):
+                    rows = slice(group * GROUP + piece * 16, group * GROUP + piece * 16 + 16)
+                    deltas = [target_ref[axis_c, rows, :] - places[tile][axis_c] for axis_c in range(3)]
+                    for part, entry in enumerate(green_terms(*deltas)):
+                        high, rest = split3(entry, part >= 2)
+                        for level, value in enumerate((high,) + rest):
+                            start = group * depth + (level * 4 + part - (2 if level == 2 else 0)) * GROUP + piece * 16
+                            green_ref[tile, start : start + 16, :] = value
+            rows = slice(group * depth, (group + 1) * depth)
+            sums = dot_t(
+                jnp.concatenate([green_ref[tile, rows, :] for tile in range(tiles)], axis=1),
+                jnp.concatenate([feature_ref[tile] for tile in range(tiles)], axis=1),
+            )
+            out_ref[rows, :] = sums if before_ref is None else before_ref[rows, :] + sums
+
+    chunk(0, before_ref)
+    if chips > CHUNK_TILES:
+        pl.loop(1, chips // CHUNK_TILES)(lambda step: chunk(step, out_ref))
 
 
 def split3(value, three=True):
@@ -239,13 +252,11 @@
 
 
 def first_pair_kernel(chips, centre_ref, target_ref, source_ref, out_ref, green_ref, feature_ref):
-    out_ref[...] = jnp.zeros_like(out_ref)
-    accumulate_pairs(chips, centre_ref, target_ref, source_ref, out_ref, green_ref, feature_ref)
+    accumulate_pairs(chips, centre_ref, target_ref, (source_ref,), None, out_ref, green_ref, feature_ref)
 
 
 def next_pair_kernel(chips, centre_ref, target_ref, source_ref, before_ref, out_ref, green_ref, feature_ref):
-    out_ref[...] = before_ref[...]
-    accumulate_pairs(chips, centre_ref, target_ref, source_ref, out_ref, green_ref, feature_ref)
+    accumulate_pairs(chips, centre_ref, target_ref, (source_ref,), before_ref, out_ref, green_ref, feature_ref)
 
 
 def complex_rows(real, imag):
@@ -257,13 +268,19 @@
 
 
 def last_pair_kernel(
-    chips, centre_ref, target_ref, source_ref, first_ref, place_ref, base_ref, out_ref, sum_ref, green_ref, feature_ref
+    chips, centre_ref, target_ref, side_ref, near_ref, first_ref, place_ref, base_ref, out_ref, sum_ref, green_ref,
+    feature_ref,
 ):
-    sum_ref[...] = first_ref[...]
-    accumulate_pairs(chips, centre_ref, target_ref, source_ref, sum_ref, green_ref, feature_ref)
+    accumulate_pairs(chips, centre_ref, target_ref, (side_ref, near_ref), first_ref, sum_ref, green_ref, feature_ref)
     targets = place_ref.shape[1]
-    raw = sum_ref[0 : 4 * targets, :] + sum_ref[4 * targets : 8 * targets, :]
-    raw = jnp.concatenate([raw[: 2 * targets], raw[2 * targets :] + sum_ref[8 * targets :, :]], axis=0)
+
+    def level(entry, part):
+        starts = [group * 10 * GROUP + (entry * 4 + part) * GROUP for group in range(targets // GROUP)]
+        return jnp.concatenate([sum_ref[start : start + GROUP, :] for start in starts], axis=0)
+
+    raw = jnp.concatenate(
+        [level(0, part) + level(1, part) + (level(2, part - 2) if part >= 2 else 0.0) for part in range(4)], axis=0
+    )
     raw = jnp.transpose(raw, (1, 0))
     raw = raw[0:FEATURES] + raw[FEATURES : 2 * FEATURES] + raw[2 * FEATURES :]
     near_re, near_im, far_re, far_im = [raw[:, part * targets : (part + 1) * targets] for part in range(4)]
@@ -307,19 +324,19 @@
         out_ref[1, axis_c] = result[2:4]
 
 
-def kernel_call(body, outs, operands, scratch=(), flops=100_000, loads=False):
+def kernel_call(body, outs, operands, scratch=(), flops=100_000, loads=()):
     single = not isinstance(outs, tuple)
     vmem = pl.BlockSpec(memory_space=pltpu.VMEM)
-    source = pl.BlockSpec(memory_space=pltpu.HBM) if loads else vmem
+    hbm = pl.BlockSpec(memory_space=pltpu.HBM)
     return pl.pallas_call(
         body,
         out_shape=outs,
-        in_specs=[source] * len(operands),
+        in_specs=[vmem] * len(operands) + [hbm] * len(loads),
         out_specs=vmem if single else (vmem,) * len(outs),
         scratch_shapes=list(scratch),
         cost_estimate=pl.CostEstimate(flops=flops, bytes_accessed=100_000, transcendentals=0),
         compiler_params=pltpu.CompilerParams(vmem_limit_bytes=12 * 1024 * 1024),
-    )(*operands)
+    )(*operands, *loads)
 
 
 def on_device(devices, positions, moments, inv_polar_re, inv_polar_im, mode_field, mode_detune, mode_width):
@@ -339,22 +356,18 @@
     mode_rows = mode_field.reshape(6 * targets, modes)
     moments_other = exchange(moments, 1)
     positions_other = exchange(positions, 1)
-    inputs = tuple(pltpu.with_memory_space_constraint(value, pltpu.HBM) for value in (
-        mode_rows,
-        moments,
-        positions,
-        mode_detune[None],
-        mode_width[None],
-        inv_polar_re[None],
-        inv_polar_im[None],
-    ))
-    amp, mode_rows, moments, positions, detune, width, polar_re, polar_im = kernel_call(
+
+    def in_hbm(*values):
+        return tuple(pltpu.with_memory_space_constraint(value, pltpu.HBM) for value in values)
+
+    inputs = in_hbm(mode_rows, moments, positions)
+    amp, mode_rows, moments, positions = kernel_call(
         project_kernel,
         (shape(AMP_ROWS, LANES),) + tuple(like(value) for value in inputs),
-        inputs,
-        [pltpu.SemaphoreType.DMA((2,)), pltpu.SemaphoreType.DMA((6,))],
+        (),
+        [pltpu.SemaphoreType.DMA((PIECES,)), pltpu.SemaphoreType.DMA((2,))],
         flops=5_000_000,
-        loads=True,
+        loads=inputs,
     )
     message = kernel_call(
         join_kernel, shape(ROWS + AMP_ROWS, LANES), (moments, moments_other, positions, positions_other, amp)
@@ -370,12 +383,20 @@
             shape(AMP_ROWS, LANES),
             shape(12, targets),
         ),
-        (mode_rows, positions, moments, detune, width, polar_re, polar_im),
+        (mode_rows, positions, moments),
+        [
+            pltpu.VMEM((1, modes), jnp.float32),
+            pltpu.VMEM((1, modes), jnp.float32),
+            pltpu.VMEM((1, targets), jnp.float32),
+            pltpu.VMEM((1, targets), jnp.float32),
+            pltpu.SemaphoreType.DMA((4,)),
+        ],
         flops=5_000_000,
+        loads=in_hbm(mode_detune[None], mode_width[None], inv_polar_re[None], inv_polar_im[None]),
     )
     distance = devices // 2
     while distance > 4:
-        steps = (distance ^ 1, (3 * distance // 2) ^ 1, distance // 2) if distance > 8 else (distance ^ 1,)
+        steps = ((3 * distance // 2) ^ 1, distance ^ 1, distance // 2) if distance > 8 else (distance ^ 1,)
         arrived = [exchange(message, step) for step in steps]
         rows = message.shape[0] - AMP_ROWS
         message = kernel_call(merge_kernel, shape((1 + len(steps)) * rows + AMP_ROWS, LANES), (message, *arrived))
@@ -385,28 +406,28 @@
     side = exchange(message, 4 ^ 1)
     near = exchange(message, 2 ^ 1)
     sums = shape(10 * targets, 3 * FEATURES)
-    scratch = [
-        pltpu.VMEM((CHUNK_TILES, 10 * targets, LANES), jnp.bfloat16),
-        pltpu.VMEM((CHUNK_TILES, 3 * FEATURES, LANES), jnp.bfloat16),
-    ]
-
-    def pair(kernel, source, *more, out=sums, extra=()):
+
+    def pair(kernel, sources, *more, out=sums, extra=()):
+        tiles = CHUNK_TILES * len(sources)
         return kernel_call(
             functools.partial(kernel, chips),
             out,
-            (centre, columns, source) + more,
-            list(extra) + scratch,
+            (centre, columns) + sources + more,
+            list(extra)
+            + [
+                pltpu.VMEM((tiles, 10 * targets, LANES), jnp.bfloat16),
+                pltpu.VMEM((tiles, 3 * FEATURES, LANES), jnp.bfloat16),
+            ],
             flops=20_000_000,
         )
 
-    partial_sums = pair(first_pair_kernel, message)
-    partial_sums = pair(next_pair_kernel, diagonal, partial_sums)
+    partial_sums = pair(first_pair_kernel, (message,))
+    partial_sums = pair(next_pair_kernel, (diagonal,), partial_sums)
     mine = kernel_call(total_kernel, shape(AMP_ROWS, LANES), (message, diagonal, side, near))
     other = exchange(mine, 1)
-    partial_sums = pair(next_pair_kernel, side, partial_sums)
     rest = pair(
         last_pair_kernel,
-        near,
+        (side, near),
         partial_sums,
         positions,
         base,

time: 22.2 us -> 22.4 us (level)
  Pallas kernels: 5.95 us -> 6.3 us
    pallas_call x10 -> x9, Pallas kernels: 5.95 us -> 6.3 us  [kernel_call(): pl.pallas_call(body, out_shape=outs, in_specs=[vmem] * len(operands) + [h...]
  transfers between devices with their start and end apart: 9 -> 9, of which waited for: 4 -> 5; matrix products, arithmetic and copies ran while one was open for 0% -> 0% of each run, Pallas kernels for 22% -> 24%
where the time goes in v3:
time: 22.4 us; the launch traced here: 22.2 us
  starting transfers between devices  9.41 us (42%)
  waiting for transfers between devices  6.47 us (29%)
  Pallas kernels  6.3 us (28%)
    ppermute x9, starting transfers between devices, exchange(): lax.ppermute(value, AXES, [(i, i ^ distance) for i in range(devices)])  9.41 us
    ppermute x9, waiting for transfers between devices, exchange(): lax.ppermute(value, AXES, [(i, i ^ distance) for i in range(devices)])  6.47 us
    pallas_call x9, Pallas kernels, kernel_call(): pl.pallas_call(body, out_shape=outs, in_specs=[vmem] * len(operands) + [h...  6.3 us
  transfers between devices with their start and end apart: 9, of which 5 were waited for; matrix products, arithmetic and copies ran while one was open for 0% of the time, Pallas kernels for 24%

profile of v3, /device:TPU:0, one launch (start us, length us, event | category | flops | bytes accessed | tf_op | source)
XLA Modules:
  0.0 22.2 jit_solution(15616484814798557341)
XLA Ops:
  0.0 0.5 %collective-permute-start = (f32[2,3,2,64]{3,2,1,0:T(2,128)}, f32[2,3,2,64]{3,2,1,0:T(2,128)S(1)}, u32[]{:S(2)}, u32[]{:S(2)}) collective-permute-start(f32[2,3,2,64]{3,2,1,0:T(2,128)} %bitcast.8), channel_id=1, source_target_pairs={{0,1},{1,0},{2,3},{3,2},{4,5},{5,4},{6,7},{7,6},{8,9},{9,8},{10,11... | collective-permute-start | bytes 9224 | tf_op jit(solution)/shard_map/ppermute | solution.py:350
  0.5 0.0 collective-permute-start.1
  0.5 1.4 %shard_map.73 = (f32[16,128]{1,0:T(8,128)S(1)}, f32[384,512]{1,0:T(8,128)S(1)}, f32[2,3,2,64]{3,2,1,0:T(2,128)S(1)}, f32[3,64]{1,0:T(4,128)S(1)}) custom-call(f32[384,512]{1,0:T(8,128)} %bitcast.7, f32[2,3,2,64]{3,2,1,0:T(2,128)} %bitcast.9, f32[3,64]{1,0:T(4,128)} %place_hbm.1), custom_call_target="tpu_custom_call" | custom-call | flops 5000000 | bytes 100000 | tf_op jit(solution)/shard_map/pallas_call | solution.py:331
  1.9 0.0 collective-permute-done.1.place_other_ref
  2.0 0.0 collective-permute-done.moment_other_ref
  2.0 0.1 shard_map.74.refs_0_
  2.0 4.7 %collective-permute-start.2 = (f32[32,128]{1,0:T(8,128)S(1)}, f32[32,128]{1,0:T(8,128)S(1)}, u32[]{:S(2)}, u32[]{:S(2)}) collective-permute-start(f32[32,128]{1,0:T(8,128)S(1)} %shard_map.74.refs_0_), channel_id=1, source_target_pairs={{0,25},{1,24},{2,27},{3,26},{4,29},{5,28},{6,31},{7,30},{8,17},{9,... | collective-permute-start | bytes 49160 | tf_op jit(solution)/shard_map/ppermute | solution.py:350
  6.7 0.0 collective-permute-start.3
  6.7 0.6 %collective-permute-start.4 = (f32[32,128]{1,0:T(8,128)S(1)}, f32[32,128]{1,0:T(8,128)S(1)}, u32[]{:S(2)}, u32[]{:S(2)}) collective-permute-start(f32[32,128]{1,0:T(8,128)S(1)} %shard_map.74.refs_0_), channel_id=1, source_target_pairs={{0,8},{1,9},{2,10},{3,11},{4,12},{5,13},{6,14},{7,15},{8,0},{9,1},... | collective-permute-start | bytes 49160 | tf_op jit(solution)/shard_map/ppermute | solution.py:350
  7.4 0.8 %collective-permute-done.2.refs_1_ = f32[32,128]{1,0:T(8,128)S(1)} collective-permute-done((f32[32,128]{1,0:T(8,128)S(1)}, f32[32,128]{1,0:T(8,128)S(1)}, u32[]{:S(2)}, u32[]{:S(2)}) %collective-permute-start.2) | collective-permute-done | bytes 16416 | tf_op jit(solution)/shard_map/ppermute | solution.py:350
  8.2 2.6 %collective-permute-done.3.refs_2_ = f32[32,128]{1,0:T(8,128)S(1)} collective-permute-done((f32[32,128]{1,0:T(8,128)S(1)}, f32[32,128]{1,0:T(8,128)S(1)}, u32[]{:S(2)}, u32[]{:S(2)}) %collective-permute-start.3) | collective-permute-done | bytes 16416 | tf_op jit(solution)/shard_map/ppermute | solution.py:350
  10.8 0.0 collective-permute-done.4.refs_3_
  10.8 2.5 %collective-permute-start.5 = (f32[80,128]{1,0:T(8,128)S(1)}, f32[80,128]{1,0:T(8,128)S(1)}, u32[]{:S(2)}, u32[]{:S(2)}) collective-permute-start(f32[80,128]{1,0:T(8,128)S(1)} %shard_map.75.refs_0_.source_ref), channel_id=1, source_target_pairs={{0,6},{1,7},{2,4},{3,5},{4,2},{5,3},{6,0},{7,1},{8,14},{9,15},{10,... | collective-permute-start | bytes 122888 | tf_op jit(solution)/shard_map/ppermute | solution.py:350
  13.3 0.4 %collective-permute-start.6 = (f32[80,128]{1,0:T(8,128)S(1)}, f32[80,128]{1,0:T(8,128)S(1)}, u32[]{:S(2)}, u32[]{:S(2)}) collective-permute-start(f32[80,128]{1,0:T(8,128)S(1)} %shard_map.75.refs_0_.source_ref), channel_id=1, source_target_pairs={{0,5},{1,4},{2,7},{3,6},{4,1},{5,0},{6,3},{7,2},{8,13},{9,12},{10,... | collective-permute-start | bytes 122888 | tf_op jit(solution)/shard_map/ppermute | solution.py:350
  13.7 0.4 %collective-permute-start.7 = (f32[80,128]{1,0:T(8,128)S(1)}, f32[80,128]{1,0:T(8,128)S(1)}, u32[]{:S(2)}, u32[]{:S(2)}) collective-permute-start(f32[80,128]{1,0:T(8,128)S(1)} %shard_map.75.refs_0_.source_ref), channel_id=1, source_target_pairs={{0,3},{1,2},{2,1},{3,0},{4,7},{5,6},{6,5},{7,4},{8,11},{9,10},{10,... | collective-permute-start | bytes 122888 | tf_op jit(solution)/shard_map/ppermute | solution.py:350
  14.1 1.7 %collective-permute-done.5.refs_1_.source_ref = f32[80,128]{1,0:T(8,128)S(1)} collective-permute-done((f32[80,128]{1,0:T(8,128)S(1)}, f32[80,128]{1,0:T(8,128)S(1)}, u32[]{:S(2)}, u32[]{:S(2)}) %collective-permute-start.5) | collective-permute-done | bytes 40992 | tf_op jit(solution)/shard_map/ppermute | solution.py:350
  15.8 1.0 %collective-permute-done.6.refs_2_.side_ref = f32[80,128]{1,0:T(8,128)S(1)} collective-permute-done((f32[80,128]{1,0:T(8,128)S(1)}, f32[80,128]{1,0:T(8,128)S(1)}, u32[]{:S(2)}, u32[]{:S(2)}) %collective-permute-start.6) | collective-permute-done | bytes 40992 | tf_op jit(solution)/shard_map/ppermute | solution.py:350
  16.8 0.3 %collective-permute-done.7.refs_3_.near_ref = f32[80,128]{1,0:T(8,128)S(1)} collective-permute-done((f32[80,128]{1,0:T(8,128)S(1)}, f32[80,128]{1,0:T(8,128)S(1)}, u32[]{:S(2)}, u32[]{:S(2)}) %collective-permute-start.7) | collective-permute-done | bytes 40992 | tf_op jit(solution)/shard_map/ppermute | solution.py:350
  17.1 0.3 %collective-permute-start.8 = (f32[16,128]{1,0:T(8,128)S(1)}, f32[16,128]{1,0:T(8,128)S(1)}, u32[]{:S(2)}, u32[]{:S(2)}) collective-permute-start(f32[16,128]{1,0:T(8,128)S(1)} %shard_map.76.mine_ref), channel_id=1, source_target_pairs={{0,1},{1,0},{2,3},{3,2},{4,5},{5,4},{6,7},{7,6},{8,9},{9,8},{10,11... | collective-permute-start | bytes 24584 | tf_op jit(solution)/shard_map/ppermute | solution.py:350
  17.4 1.0 %shard_map.77 = (bf16[512,384]{1,0:T(8,128)(2,1)S(1)}, bf16[512,384]{1,0:T(8,128)(2,1)S(1)}, f32[3,64,128]{2,1,0:T(8,128)S(1)}, f32[8,128]{1,0:T(8,128)S(1)}, f3...) custom-call(f32[384,512]{1,0:T(8,128)S(1)} %get-tuple-element.19.mode_ref, ...), custom_call_target="tpu_custom_call" | custom-call | flops 5000000 | bytes 100000 | tf_op jit(solution)/shard_map/pallas_call | solution.py:331
  18.4 0.7 %shard_map.78.before_ref = f32[640,192]{1,0:T(8,128)S(1)} custom-call(f32[8,128]{1,0:T(8,128)S(1)} %get-tuple-element.24.centre_ref, f32[3,64,128]{2,1,0:T(8,128)S(1)} %get-tuple-element.25.target_ref, f32[80,128]{1,0:T(8,128)S(1)} %shard_map.75.refs_0_.source_ref), custom_call_target="tpu_custom_call" | custom-call | flops 20000000 | bytes 100000 | tf_op jit(solution)/shard_map/pallas_call | solution.py:331
  19.1 0.7 %shard_map.79.first_ref = f32[640,192]{1,0:T(8,128)S(1)} custom-call(f32[8,128]{1,0:T(8,128)S(1)} %get-tuple-element.24.centre_ref, f32[3,64,128]{2,1,0:T(8,128)S(1)} %get-tuple-element.25.target_ref, f32[80,128]{1,0:T(8,128)S(1)} %collective-permute-done.5.refs_1_.source_ref, f32[640,192]{1,0:T(8,128)S(1)} %shard_map.78.before_ref), custom_call_target="tpu_custom_call" | custom-call | flops 20000000 | bytes 100000 | tf_op jit(solution)/shard_map/pallas_call | solution.py:331
  19.8 1.5 %shard_map.80.rest_ref = f32[12,64]{1,0:T(8,128)S(1)} custom-call(f32[8,128]{1,0:T(8,128)S(1)} %get-tuple-element.24.centre_ref, f32[3,64,128]{2,1,0:T(8,128)S(1)} %get-tuple-element.25.target_ref, f32[80,128]{1,0:T(8,128)S(1)} %collective-permute-done.6.refs_2_.side_ref, f32[80,128]{1,0:T(8,128)S(1)} %collective-permute-done.7.refs_3_.near_ref, ...), custom_call_target="tpu_custom_call" | custom-call | flops 20000000 | bytes 100000 | tf_op jit(solution)/shard_map/pallas_call | solution.py:331
  21.3 0.0 collective-permute-done.8.other_ref
  21.3 1.0 %shard_map.81 = f32[2,3,2,64]{3,2,1,0:T(2,128)} custom-call(f32[16,128]{1,0:T(8,128)S(1)} %shard_map.76.mine_ref, f32[16,128]{1,0:T(8,128)S(1)} %collective-permute-done.8.other_ref, bf16[512,384]{1,0:T(8,128)(2,1)S(1)} %get-tuple-element.20.high_ref, bf16[512,384]{1,0:T(8,128)(2,1)S(1)} %get-tuple-element.21.low_ref, ...), custom_call_target="tpu_custom_call" | custom-call | flops 100000 | bytes 100000 | tf_op jit(solution)/shard_map/pallas_call | solution.py:331
  (2 shorter events, 0.0 us)
Async XLA Ops:
  0.0 2.0 %collective-permute-start = (f32[2,3,2,64]{3,2,1,0:T(2,128)}, f32[2,3,2,64]{3,2,1,0:T(2,128)S(1)}, u32[]{:S(2)}, u32[]{:S(2)}) collective-permute-start(f32[2,3,2,64]{3,2,1,0:T(2,128)} %bitcast.8), channel_id=1, source_target_pairs={{0,1},{1,0},{2,3},{3,2},{4,5},{5,4},{6,7},{7,6},{8,9},{9,8},{10,11... | collective-permute-start | bytes 9224 | tf_op jit(solution)/shard_map/ppermute | solution.py:350
  0.5 1.5 %collective-permute-start.1 = (f32[3,64]{1,0:T(4,128)}, f32[3,64]{1,0:T(4,128)S(1)}, u32[]{:S(2)}, u32[]{:S(2)}) collective-permute-start(f32[3,64]{1,0:T(4,128)} %place_hbm.1), channel_id=1, source_target_pairs={{0,1},{1,0},{2,3},{3,2},{4,5},{5,4},{6,7},{7,6},{8,9},{9,8},{10,11... | collective-permute-start | bytes 2312 | tf_op jit(solution)/shard_map/ppermute | solution.py:350
  2.0 6.1 %collective-permute-start.2 = (f32[32,128]{1,0:T(8,128)S(1)}, f32[32,128]{1,0:T(8,128)S(1)}, u32[]{:S(2)}, u32[]{:S(2)}) collective-permute-start(f32[32,128]{1,0:T(8,128)S(1)} %shard_map.74.refs_0_), channel_id=1, source_target_pairs={{0,25},{1,24},{2,27},{3,26},{4,29},{5,28},{6,31},{7,30},{8,17},{9,... | collective-permute-start | bytes 49160 | tf_op jit(solution)/shard_map/ppermute | solution.py:350
  6.7 4.1 %collective-permute-start.3 = (f32[32,128]{1,0:T(8,128)S(1)}, f32[32,128]{1,0:T(8,128)S(1)}, u32[]{:S(2)}, u32[]{:S(2)}) collective-permute-start(f32[32,128]{1,0:T(8,128)S(1)} %shard_map.74.refs_0_), channel_id=1, source_target_pairs={{0,17},{1,16},{2,19},{3,18},{4,21},{5,20},{6,23},{7,22},{8,25},{9,... | collective-permute-start | bytes 49160 | tf_op jit(solution)/shard_map/ppermute | solution.py:350
  6.7 4.1 %collective-permute-start.4 = (f32[32,128]{1,0:T(8,128)S(1)}, f32[32,128]{1,0:T(8,128)S(1)}, u32[]{:S(2)}, u32[]{:S(2)}) collective-permute-start(f32[32,128]{1,0:T(8,128)S(1)} %shard_map.74.refs_0_), channel_id=1, source_target_pairs={{0,8},{1,9},{2,10},{3,11},{4,12},{5,13},{6,14},{7,15},{8,0},{9,1},... | collective-permute-start | bytes 49160 | tf_op jit(solution)/shard_map/ppermute | solution.py:350
  10.8 5.0 %collective-permute-start.5 = (f32[80,128]{1,0:T(8,128)S(1)}, f32[80,128]{1,0:T(8,128)S(1)}, u32[]{:S(2)}, u32[]{:S(2)}) collective-permute-start(f32[80,128]{1,0:T(8,128)S(1)} %shard_map.75.refs_0_.source_ref), channel_id=1, source_target_pairs={{0,6},{1,7},{2,4},{3,5},{4,2},{5,3},{6,0},{7,1},{8,14},{9,15},{10,... | collective-permute-start | bytes 122888 | tf_op jit(solution)/shard_map/ppermute | solution.py:350
  13.3 3.5 %collective-permute-start.6 = (f32[80,128]{1,0:T(8,128)S(1)}, f32[80,128]{1,0:T(8,128)S(1)}, u32[]{:S(2)}, u32[]{:S(2)}) collective-permute-start(f32[80,128]{1,0:T(8,128)S(1)} %shard_map.75.refs_0_.source_ref), channel_id=1, source_target_pairs={{0,5},{1,4},{2,7},{3,6},{4,1},{5,0},{6,3},{7,2},{8,13},{9,12},{10,... | collective-permute-start | bytes 122888 | tf_op jit(solution)/shard_map/ppermute | solution.py:350
  13.7 3.4 %collective-permute-start.7 = (f32[80,128]{1,0:T(8,128)S(1)}, f32[80,128]{1,0:T(8,128)S(1)}, u32[]{:S(2)}, u32[]{:S(2)}) collective-permute-start(f32[80,128]{1,0:T(8,128)S(1)} %shard_map.75.refs_0_.source_ref), channel_id=1, source_target_pairs={{0,3},{1,2},{2,1},{3,0},{4,7},{5,6},{6,5},{7,4},{8,11},{9,10},{10,... | collective-permute-start | bytes 122888 | tf_op jit(solution)/shard_map/ppermute | solution.py:350
  17.1 4.1 %collective-permute-start.8 = (f32[16,128]{1,0:T(8,128)S(1)}, f32[16,128]{1,0:T(8,128)S(1)}, u32[]{:S(2)}, u32[]{:S(2)}) collective-permute-start(f32[16,128]{1,0:T(8,128)S(1)} %shard_map.76.mine_ref), channel_id=1, source_target_pairs={{0,1},{1,0},{2,3},{3,2},{4,5},{5,4},{6,7},{7,6},{8,9},{9,8},{10,11... | collective-permute-start | bytes 24584 | tf_op jit(solution)/shard_map/ppermute | solution.py:350

commit v4 on v3

--- a/solution.py
+++ b/solution.py
@@ -19,7 +19,6 @@
 PIECES = 3
 AMP_ROWS = 16
 FEATURES = 64
-GROUP = 32
 
 PI_HIGH = 3.140625
 PI_LOW = math.pi - PI_HIGH
@@ -191,10 +190,8 @@
 
 
 def accumulate_pairs(chips, centre_ref, target_ref, source_refs, before_ref, out_ref, green_ref, feature_ref):
-    groups = target_ref.shape[1] // GROUP
-    depth = 10 * GROUP
+    targets = target_ref.shape[1]
     centre = [centre_ref[axis_c : axis_c + 1, 0:1] for axis_c in range(3)]
-
     tiles = CHUNK_TILES * len(source_refs)
 
     def chunk(step, before_ref):
@@ -220,22 +217,33 @@
             feature_ref[tile, 0:FEATURES, :] = high
             feature_ref[tile, FEATURES : 2 * FEATURES, :] = middle
             feature_ref[tile, 2 * FEATURES :, :] = low
-        for group in range(groups):
-            for tile in range(tiles):
-                for piece in range(GROUP // 16):
-                    rows = slice(group * GROUP + piece * 16, group * GROUP + piece * 16 + 16)
+        for start in range(0, tiles, 2):
+            pair_tiles = range(start, start + 2)
+            for tile in pair_tiles:
+                for group in range(targets // 16):
+                    rows = slice(group * 16, group * 16 + 16)
                     deltas = [target_ref[axis_c, rows, :] - places[tile][axis_c] for axis_c in range(3)]
                     for part, entry in enumerate(green_terms(*deltas)):
                         high, rest = split3(entry, part >= 2)
                         for level, value in enumerate((high,) + rest):
-                            start = group * depth + (level * 4 + part - (2 if level == 2 else 0)) * GROUP + piece * 16
-                            green_ref[tile, start : start + 16, :] = value
-            rows = slice(group * depth, (group + 1) * depth)
-            sums = dot_t(
-                jnp.concatenate([green_ref[tile, rows, :] for tile in range(tiles)], axis=1),
-                jnp.concatenate([feature_ref[tile] for tile in range(tiles)], axis=1),
+                            row = (level * 4 + part - (2 if level == 2 else 0)) * targets + group * 16
+                            green_ref[tile, row : row + 16, :] = value
+
+            def green(first, last):
+                return jnp.concatenate([green_ref[tile, first * targets : last * targets, :] for tile in pair_tiles], axis=1)
+
+            features = jnp.concatenate([feature_ref[tile] for tile in pair_tiles], axis=1)
+            high = dot_t(features, green(0, 4))
+            middle = dot_t(features[: 2 * FEATURES], green(4, 8))
+            low = dot_t(features[:FEATURES], green(8, 10))
+            sums = (high[:FEATURES] + high[FEATURES : 2 * FEATURES] + high[2 * FEATURES :]) + (
+                middle[:FEATURES] + middle[FEATURES:]
             )
-            out_ref[rows, :] = sums if before_ref is None else before_ref[rows, :] + sums
+            half = 2 * targets
+            for lanes, extra in ((slice(0, half), 0.0), (slice(half, 2 * half), low)):
+                value = sums[:, lanes] + extra
+                out_ref[:, lanes] = value if before_ref is None else before_ref[:, lanes] + value
+            before_ref = out_ref
 
     chunk(0, before_ref)
     if chips > CHUNK_TILES:
@@ -273,16 +281,7 @@
 ):
     accumulate_pairs(chips, centre_ref, target_ref, (side_ref, near_ref), first_ref, sum_ref, green_ref, feature_ref)
     targets = place_ref.shape[1]
-
-    def level(entry, part):
-        starts = [group * 10 * GROUP + (entry * 4 + part) * GROUP for group in range(targets // GROUP)]
-        return jnp.concatenate([sum_ref[start : start + GROUP, :] for start in starts], axis=0)
-
-    raw = jnp.concatenate(
-        [level(0, part) + level(1, part) + (level(2, part - 2) if part >= 2 else 0.0) for part in range(4)], axis=0
-    )
-    raw = jnp.transpose(raw, (1, 0))
-    raw = raw[0:FEATURES] + raw[FEATURES : 2 * FEATURES] + raw[2 * FEATURES :]
+    raw = sum_ref[...]
     near_re, near_im, far_re, far_im = [raw[:, part * targets : (part + 1) * targets] for part in range(4)]
     local = [place_ref[axis_c : axis_c + 1, :] - centre_ref[axis_c : axis_c + 1, 0:1] for axis_c in range(3)]
 
@@ -405,7 +404,7 @@
     diagonal = exchange(message, 6)
     side = exchange(message, 4 ^ 1)
     near = exchange(message, 2 ^ 1)
-    sums = shape(10 * targets, 3 * FEATURES)
+    sums = shape(FEATURES, 4 * targets)
 
     def pair(kernel, sources, *more, out=sums, extra=()):
         tiles = CHUNK_TILES * len(sources)

time: 22.4 us -> 22.3 us (level)
  transfers between devices with their start and end apart: 9 -> 9, of which waited for: 5 -> 5; matrix products, arithmetic and copies ran while one was open for 0% -> 0% of each run, Pallas kernels for 24% -> 23%
where the time goes in v4:
time: 22.3 us; the launch traced here: 22.1 us
  starting transfers between devices  9.4 us (42%)
  waiting for transfers between devices  6.46 us (29%)
  Pallas kernels  6.18 us (28%)
    ppermute x9, starting transfers between devices, exchange(): lax.ppermute(value, AXES, [(i, i ^ distance) for i in range(devices)])  9.4 us
    ppermute x9, waiting for transfers between devices, exchange(): lax.ppermute(value, AXES, [(i, i ^ distance) for i in range(devices)])  6.46 us
    pallas_call x9, Pallas kernels, kernel_call(): pl.pallas_call(body, out_shape=outs, in_specs=[vmem] * len(operands) + [h...  6.18 us
  transfers between devices with their start and end apart: 9, of which 5 were waited for; matrix products, arithmetic and copies ran while one was open for 0% of the time, Pallas kernels for 23%

profile of v4, /device:TPU:0, one launch (start us, length us, event | category | flops | bytes accessed | tf_op | source)
XLA Modules:
  0.0 22.1 jit_solution(6548309725957140898)
XLA Ops:
  0.0 0.5 %collective-permute-start = (f32[2,3,2,64]{3,2,1,0:T(2,128)}, f32[2,3,2,64]{3,2,1,0:T(2,128)S(1)}, u32[]{:S(2)}, u32[]{:S(2)}) collective-permute-start(f32[2,3,2,64]{3,2,1,0:T(2,128)} %bitcast.8), channel_id=1, source_target_pairs={{0,1},{1,0},{2,3},{3,2},{4,5},{5,4},{6,7},{7,6},{8,9},{9,8},{10,11... | collective-permute-start | bytes 9224 | tf_op jit(solution)/shard_map/ppermute | solution.py:349
  0.5 0.0 collective-permute-start.1
  0.5 1.4 %shard_map.73 = (f32[16,128]{1,0:T(8,128)S(1)}, f32[384,512]{1,0:T(8,128)S(1)}, f32[2,3,2,64]{3,2,1,0:T(2,128)S(1)}, f32[3,64]{1,0:T(4,128)S(1)}) custom-call(f32[384,512]{1,0:T(8,128)} %bitcast.7, f32[2,3,2,64]{3,2,1,0:T(2,128)} %bitcast.9, f32[3,64]{1,0:T(4,128)} %place_hbm.1), custom_call_target="tpu_custom_call" | custom-call | flops 5000000 | bytes 100000 | tf_op jit(solution)/shard_map/pallas_call | solution.py:330
  1.9 0.0 collective-permute-done.1.place_other_ref
  2.0 0.0 collective-permute-done.moment_other_ref
  2.0 0.1 shard_map.74.refs_0_
  2.0 4.7 %collective-permute-start.2 = (f32[32,128]{1,0:T(8,128)S(1)}, f32[32,128]{1,0:T(8,128)S(1)}, u32[]{:S(2)}, u32[]{:S(2)}) collective-permute-start(f32[32,128]{1,0:T(8,128)S(1)} %shard_map.74.refs_0_), channel_id=1, source_target_pairs={{0,25},{1,24},{2,27},{3,26},{4,29},{5,28},{6,31},{7,30},{8,17},{9,... | collective-permute-start | bytes 49160 | tf_op jit(solution)/shard_map/ppermute | solution.py:349
  6.7 0.0 collective-permute-start.3
  6.7 0.6 %collective-permute-start.4 = (f32[32,128]{1,0:T(8,128)S(1)}, f32[32,128]{1,0:T(8,128)S(1)}, u32[]{:S(2)}, u32[]{:S(2)}) collective-permute-start(f32[32,128]{1,0:T(8,128)S(1)} %shard_map.74.refs_0_), channel_id=1, source_target_pairs={{0,8},{1,9},{2,10},{3,11},{4,12},{5,13},{6,14},{7,15},{8,0},{9,1},... | collective-permute-start | bytes 49160 | tf_op jit(solution)/shard_map/ppermute | solution.py:349
  7.4 0.8 %collective-permute-done.2.refs_1_ = f32[32,128]{1,0:T(8,128)S(1)} collective-permute-done((f32[32,128]{1,0:T(8,128)S(1)}, f32[32,128]{1,0:T(8,128)S(1)}, u32[]{:S(2)}, u32[]{:S(2)}) %collective-permute-start.2) | collective-permute-done | bytes 16416 | tf_op jit(solution)/shard_map/ppermute | solution.py:349
  8.2 2.6 %collective-permute-done.3.refs_2_ = f32[32,128]{1,0:T(8,128)S(1)} collective-permute-done((f32[32,128]{1,0:T(8,128)S(1)}, f32[32,128]{1,0:T(8,128)S(1)}, u32[]{:S(2)}, u32[]{:S(2)}) %collective-permute-start.3) | collective-permute-done | bytes 16416 | tf_op jit(solution)/shard_map/ppermute | solution.py:349
  10.8 0.0 collective-permute-done.4.refs_3_
  10.8 2.5 %collective-permute-start.5 = (f32[80,128]{1,0:T(8,128)S(1)}, f32[80,128]{1,0:T(8,128)S(1)}, u32[]{:S(2)}, u32[]{:S(2)}) collective-permute-start(f32[80,128]{1,0:T(8,128)S(1)} %shard_map.75.refs_0_.source_ref), channel_id=1, source_target_pairs={{0,6},{1,7},{2,4},{3,5},{4,2},{5,3},{6,0},{7,1},{8,14},{9,15},{10,... | collective-permute-start | bytes 122888 | tf_op jit(solution)/shard_map/ppermute | solution.py:349
  13.3 0.4 %collective-permute-start.6 = (f32[80,128]{1,0:T(8,128)S(1)}, f32[80,128]{1,0:T(8,128)S(1)}, u32[]{:S(2)}, u32[]{:S(2)}) collective-permute-start(f32[80,128]{1,0:T(8,128)S(1)} %shard_map.75.refs_0_.source_ref), channel_id=1, source_target_pairs={{0,5},{1,4},{2,7},{3,6},{4,1},{5,0},{6,3},{7,2},{8,13},{9,12},{10,... | collective-permute-start | bytes 122888 | tf_op jit(solution)/shard_map/ppermute | solution.py:349
  13.7 0.4 %collective-permute-start.7 = (f32[80,128]{1,0:T(8,128)S(1)}, f32[80,128]{1,0:T(8,128)S(1)}, u32[]{:S(2)}, u32[]{:S(2)}) collective-permute-start(f32[80,128]{1,0:T(8,128)S(1)} %shard_map.75.refs_0_.source_ref), channel_id=1, source_target_pairs={{0,3},{1,2},{2,1},{3,0},{4,7},{5,6},{6,5},{7,4},{8,11},{9,10},{10,... | collective-permute-start | bytes 122888 | tf_op jit(solution)/shard_map/ppermute | solution.py:349
  14.1 1.7 %collective-permute-done.5.refs_1_.source_ref = f32[80,128]{1,0:T(8,128)S(1)} collective-permute-done((f32[80,128]{1,0:T(8,128)S(1)}, f32[80,128]{1,0:T(8,128)S(1)}, u32[]{:S(2)}, u32[]{:S(2)}) %collective-permute-start.5) | collective-permute-done | bytes 40992 | tf_op jit(solution)/shard_map/ppermute | solution.py:349
  15.8 1.0 %collective-permute-done.6.refs_2_.side_ref = f32[80,128]{1,0:T(8,128)S(1)} collective-permute-done((f32[80,128]{1,0:T(8,128)S(1)}, f32[80,128]{1,0:T(8,128)S(1)}, u32[]{:S(2)}, u32[]{:S(2)}) %collective-permute-start.6) | collective-permute-done | bytes 40992 | tf_op jit(solution)/shard_map/ppermute | solution.py:349
  16.8 0.3 %collective-permute-done.7.refs_3_.near_ref = f32[80,128]{1,0:T(8,128)S(1)} collective-permute-done((f32[80,128]{1,0:T(8,128)S(1)}, f32[80,128]{1,0:T(8,128)S(1)}, u32[]{:S(2)}, u32[]{:S(2)}) %collective-permute-start.7) | collective-permute-done | bytes 40992 | tf_op jit(solution)/shard_map/ppermute | solution.py:349
  17.1 0.3 %collective-permute-start.8 = (f32[16,128]{1,0:T(8,128)S(1)}, f32[16,128]{1,0:T(8,128)S(1)}, u32[]{:S(2)}, u32[]{:S(2)}) collective-permute-start(f32[16,128]{1,0:T(8,128)S(1)} %shard_map.76.mine_ref), channel_id=1, source_target_pairs={{0,1},{1,0},{2,3},{3,2},{4,5},{5,4},{6,7},{7,6},{8,9},{9,8},{10,11... | collective-permute-start | bytes 24584 | tf_op jit(solution)/shard_map/ppermute | solution.py:349
  17.4 1.0 %shard_map.77 = (bf16[512,384]{1,0:T(8,128)(2,1)S(1)}, bf16[512,384]{1,0:T(8,128)(2,1)S(1)}, f32[3,64,128]{2,1,0:T(8,128)S(1)}, f32[8,128]{1,0:T(8,128)S(1)}, f3...) custom-call(f32[384,512]{1,0:T(8,128)S(1)} %get-tuple-element.19.mode_ref, ...), custom_call_target="tpu_custom_call" | custom-call | flops 5000000 | bytes 100000 | tf_op jit(solution)/shard_map/pallas_call | solution.py:330
  18.4 0.7 %shard_map.78.before_ref = f32[64,256]{1,0:T(8,128)S(1)} custom-call(f32[8,128]{1,0:T(8,128)S(1)} %get-tuple-element.24.centre_ref, f32[3,64,128]{2,1,0:T(8,128)S(1)} %get-tuple-element.25.target_ref, f32[80,128]{1,0:T(8,128)S(1)} %shard_map.75.refs_0_.source_ref), custom_call_target="tpu_custom_call" | custom-call | flops 20000000 | bytes 100000 | tf_op jit(solution)/shard_map/pallas_call | solution.py:330
  19.1 0.7 %shard_map.79.first_ref = f32[64,256]{1,0:T(8,128)S(1)} custom-call(f32[8,128]{1,0:T(8,128)S(1)} %get-tuple-element.24.centre_ref, f32[3,64,128]{2,1,0:T(8,128)S(1)} %get-tuple-element.25.target_ref, f32[80,128]{1,0:T(8,128)S(1)} %collective-permute-done.5.refs_1_.source_ref, f32[64,256]{1,0:T(8,128)S(1)} %shard_map.78.before_ref), custom_call_target="tpu_custom_call" | custom-call | flops 20000000 | bytes 100000 | tf_op jit(solution)/shard_map/pallas_call | solution.py:330
  19.8 1.3 %shard_map.80.rest_ref = f32[12,64]{1,0:T(8,128)S(1)} custom-call(f32[8,128]{1,0:T(8,128)S(1)} %get-tuple-element.24.centre_ref, f32[3,64,128]{2,1,0:T(8,128)S(1)} %get-tuple-element.25.target_ref, f32[80,128]{1,0:T(8,128)S(1)} %collective-permute-done.6.refs_2_.side_ref, f32[80,128]{1,0:T(8,128)S(1)} %collective-permute-done.7.refs_3_.near_ref, ...), custom_call_target="tpu_custom_call" | custom-call | flops 20000000 | bytes 100000 | tf_op jit(solution)/shard_map/pallas_call | solution.py:330
  21.1 0.0 collective-permute-done.8.other_ref
  21.1 1.0 %shard_map.81 = f32[2,3,2,64]{3,2,1,0:T(2,128)} custom-call(f32[16,128]{1,0:T(8,128)S(1)} %shard_map.76.mine_ref, f32[16,128]{1,0:T(8,128)S(1)} %collective-permute-done.8.other_ref, bf16[512,384]{1,0:T(8,128)(2,1)S(1)} %get-tuple-element.20.high_ref, bf16[512,384]{1,0:T(8,128)(2,1)S(1)} %get-tuple-element.21.low_ref, ...), custom_call_target="tpu_custom_call" | custom-call | flops 100000 | bytes 100000 | tf_op jit(solution)/shard_map/pallas_call | solution.py:330
  (2 shorter events, 0.0 us)
Async XLA Ops:
  0.0 2.0 %collective-permute-start = (f32[2,3,2,64]{3,2,1,0:T(2,128)}, f32[2,3,2,64]{3,2,1,0:T(2,128)S(1)}, u32[]{:S(2)}, u32[]{:S(2)}) collective-permute-start(f32[2,3,2,64]{3,2,1,0:T(2,128)} %bitcast.8), channel_id=1, source_target_pairs={{0,1},{1,0},{2,3},{3,2},{4,5},{5,4},{6,7},{7,6},{8,9},{9,8},{10,11... | collective-permute-start | bytes 9224 | tf_op jit(solution)/shard_map/ppermute | solution.py:349
  0.5 1.5 %collective-permute-start.1 = (f32[3,64]{1,0:T(4,128)}, f32[3,64]{1,0:T(4,128)S(1)}, u32[]{:S(2)}, u32[]{:S(2)}) collective-permute-start(f32[3,64]{1,0:T(4,128)} %place_hbm.1), channel_id=1, source_target_pairs={{0,1},{1,0},{2,3},{3,2},{4,5},{5,4},{6,7},{7,6},{8,9},{9,8},{10,11... | collective-permute-start | bytes 2312 | tf_op jit(solution)/shard_map/ppermute | solution.py:349
  2.0 6.1 %collective-permute-start.2 = (f32[32,128]{1,0:T(8,128)S(1)}, f32[32,128]{1,0:T(8,128)S(1)}, u32[]{:S(2)}, u32[]{:S(2)}) collective-permute-start(f32[32,128]{1,0:T(8,128)S(1)} %shard_map.74.refs_0_), channel_id=1, source_target_pairs={{0,25},{1,24},{2,27},{3,26},{4,29},{5,28},{6,31},{7,30},{8,17},{9,... | collective-permute-start | bytes 49160 | tf_op jit(solution)/shard_map/ppermute | solution.py:349
  6.7 4.1 %collective-permute-start.3 = (f32[32,128]{1,0:T(8,128)S(1)}, f32[32,128]{1,0:T(8,128)S(1)}, u32[]{:S(2)}, u32[]{:S(2)}) collective-permute-start(f32[32,128]{1,0:T(8,128)S(1)} %shard_map.74.refs_0_), channel_id=1, source_target_pairs={{0,17},{1,16},{2,19},{3,18},{4,21},{5,20},{6,23},{7,22},{8,25},{9,... | collective-permute-start | bytes 49160 | tf_op jit(solution)/shard_map/ppermute | solution.py:349
  6.7 4.1 %collective-permute-start.4 = (f32[32,128]{1,0:T(8,128)S(1)}, f32[32,128]{1,0:T(8,128)S(1)}, u32[]{:S(2)}, u32[]{:S(2)}) collective-permute-start(f32[32,128]{1,0:T(8,128)S(1)} %shard_map.74.refs_0_), channel_id=1, source_target_pairs={{0,8},{1,9},{2,10},{3,11},{4,12},{5,13},{6,14},{7,15},{8,0},{9,1},... | collective-permute-start | bytes 49160 | tf_op jit(solution)/shard_map/ppermute | solution.py:349
  10.8 5.0 %collective-permute-start.5 = (f32[80,128]{1,0:T(8,128)S(1)}, f32[80,128]{1,0:T(8,128)S(1)}, u32[]{:S(2)}, u32[]{:S(2)}) collective-permute-start(f32[80,128]{1,0:T(8,128)S(1)} %shard_map.75.refs_0_.source_ref), channel_id=1, source_target_pairs={{0,6},{1,7},{2,4},{3,5},{4,2},{5,3},{6,0},{7,1},{8,14},{9,15},{10,... | collective-permute-start | bytes 122888 | tf_op jit(solution)/shard_map/ppermute | solution.py:349
  13.3 3.5 %collective-permute-start.6 = (f32[80,128]{1,0:T(8,128)S(1)}, f32[80,128]{1,0:T(8,128)S(1)}, u32[]{:S(2)}, u32[]{:S(2)}) collective-permute-start(f32[80,128]{1,0:T(8,128)S(1)} %shard_map.75.refs_0_.source_ref), channel_id=1, source_target_pairs={{0,5},{1,4},{2,7},{3,6},{4,1},{5,0},{6,3},{7,2},{8,13},{9,12},{10,... | collective-permute-start | bytes 122888 | tf_op jit(solution)/shard_map/ppermute | solution.py:349
  13.7 3.4 %collective-permute-start.7 = (f32[80,128]{1,0:T(8,128)S(1)}, f32[80,128]{1,0:T(8,128)S(1)}, u32[]{:S(2)}, u32[]{:S(2)}) collective-permute-start(f32[80,128]{1,0:T(8,128)S(1)} %shard_map.75.refs_0_.source_ref), channel_id=1, source_target_pairs={{0,3},{1,2},{2,1},{3,0},{4,7},{5,6},{6,5},{7,4},{8,11},{9,10},{10,... | collective-permute-start | bytes 122888 | tf_op jit(solution)/shard_map/ppermute | solution.py:349
  17.1 4.0 %collective-permute-start.8 = (f32[16,128]{1,0:T(8,128)S(1)}, f32[16,128]{1,0:T(8,128)S(1)}, u32[]{:S(2)}, u32[]{:S(2)}) collective-permute-start(f32[16,128]{1,0:T(8,128)S(1)} %shard_map.76.mine_ref), channel_id=1, source_target_pairs={{0,1},{1,0},{2,3},{3,2},{4,5},{5,4},{6,7},{7,6},{8,9},{9,8},{10,11... | collective-permute-start | bytes 24584 | tf_op jit(solution)/shard_map/ppermute | solution.py:349

commit v5 on v4

--- a/solution.py
+++ b/solution.py
@@ -195,30 +195,30 @@
     tiles = CHUNK_TILES * len(source_refs)
 
     def chunk(step, before_ref):
-        places = []
-        for tile in range(tiles):
-            base = (step * CHUNK_TILES + tile % CHUNK_TILES) * ROWS
-            if not isinstance(base, int):
-                base = pl.multiple_of(base, ROWS)
-            block = source_refs[tile // CHUNK_TILES][pl.ds(base, ROWS), :]
-            place = [block[12 + axis_c : 13 + axis_c, :] for axis_c in range(3)]
-            places.append([jnp.broadcast_to(row, (16, LANES)) for row in place])
-            local = [place[axis_c] - centre[axis_c] for axis_c in range(3)]
-            moment = [block[4 * axis_c : 4 * axis_c + 4, :] for axis_c in range(3)]
-            along = moment[0] * local[0] + moment[1] * local[1] + moment[2] * local[2]
-            features = jnp.concatenate(
-                [block[:12]]
-                + [block[:12] * local[axis_c] for axis_c in range(3)]
-                + [along * local[axis_c] for axis_c in range(3)]
-                + [jnp.zeros_like(along)],
-                axis=0,
-            )
-            high, (middle, low) = split3(features)
-            feature_ref[tile, 0:FEATURES, :] = high
-            feature_ref[tile, FEATURES : 2 * FEATURES, :] = middle
-            feature_ref[tile, 2 * FEATURES :, :] = low
         for start in range(0, tiles, 2):
             pair_tiles = range(start, start + 2)
+            places = {}
+            for tile in pair_tiles:
+                base = (step * CHUNK_TILES + tile % CHUNK_TILES) * ROWS
+                if not isinstance(base, int):
+                    base = pl.multiple_of(base, ROWS)
+                block = source_refs[tile // CHUNK_TILES][pl.ds(base, ROWS), :]
+                place = [block[12 + axis_c : 13 + axis_c, :] for axis_c in range(3)]
+                places[tile] = [jnp.broadcast_to(row, (16, LANES)) for row in place]
+                local = [place[axis_c] - centre[axis_c] for axis_c in range(3)]
+                moment = [block[4 * axis_c : 4 * axis_c + 4, :] for axis_c in range(3)]
+                along = moment[0] * local[0] + moment[1] * local[1] + moment[2] * local[2]
+                features = jnp.concatenate(
+                    [block[:12]]
+                    + [block[:12] * local[axis_c] for axis_c in range(3)]
+                    + [along * local[axis_c] for axis_c in range(3)]
+                    + [jnp.zeros_like(along)],
+                    axis=0,
+                )
+                high, (middle, low) = split3(features)
+                feature_ref[tile, 0:FEATURES, :] = high
+                feature_ref[tile, FEATURES : 2 * FEATURES, :] = middle
+                feature_ref[tile, 2 * FEATURES :, :] = low
             for tile in pair_tiles:
                 for group in range(targets // 16):
                     rows = slice(group * 16, group * 16 + 16)

time: 22.3 us -> 22.3 us (level)
  no operation moved by 1% of the time
where the time goes in v5:
time: 22.3 us; the launch traced here: 22.1 us
  starting transfers between devices  9.4 us (42%)
  waiting for transfers between devices  6.46 us (29%)
  Pallas kernels  6.18 us (28%)
    ppermute x9, starting transfers between devices, exchange(): lax.ppermute(value, AXES, [(i, i ^ distance) for i in range(devices)])  9.4 us
    ppermute x9, waiting for transfers between devices, exchange(): lax.ppermute(value, AXES, [(i, i ^ distance) for i in range(devices)])  6.46 us
    pallas_call x9, Pallas kernels, kernel_call(): pl.pallas_call(body, out_shape=outs, in_specs=[vmem] * len(operands) + [h...  6.18 us
  transfers between devices with their start and end apart: 9, of which 5 were waited for; matrix products, arithmetic and copies ran while one was open for 0% of the time, Pallas kernels for 23%

profile of v5, /device:TPU:0, one launch (start us, length us, event | category | flops | bytes accessed | tf_op | source)
XLA Modules:
  0.0 22.1 jit_solution(6548309725957140898)
XLA Ops:
  0.0 0.5 %collective-permute-start = (f32[2,3,2,64]{3,2,1,0:T(2,128)}, f32[2,3,2,64]{3,2,1,0:T(2,128)S(1)}, u32[]{:S(2)}, u32[]{:S(2)}) collective-permute-start(f32[2,3,2,64]{3,2,1,0:T(2,128)} %bitcast.8), channel_id=1, source_target_pairs={{0,1},{1,0},{2,3},{3,2},{4,5},{5,4},{6,7},{7,6},{8,9},{9,8},{10,11... | collective-permute-start | bytes 9224 | tf_op jit(solution)/shard_map/ppermute | solution.py:349
  0.5 0.0 collective-permute-start.1
  0.5 1.4 %shard_map.73 = (f32[16,128]{1,0:T(8,128)S(1)}, f32[384,512]{1,0:T(8,128)S(1)}, f32[2,3,2,64]{3,2,1,0:T(2,128)S(1)}, f32[3,64]{1,0:T(4,128)S(1)}) custom-call(f32[384,512]{1,0:T(8,128)} %bitcast.7, f32[2,3,2,64]{3,2,1,0:T(2,128)} %bitcast.9, f32[3,64]{1,0:T(4,128)} %place_hbm.1), custom_call_target="tpu_custom_call" | custom-call | flops 5000000 | bytes 100000 | tf_op jit(solution)/shard_map/pallas_call | solution.py:330
  1.9 0.0 collective-permute-done.1.place_other_ref
  2.0 0.0 collective-permute-done.moment_other_ref
  2.0 0.1 shard_map.74.refs_0_
  2.0 4.7 %collective-permute-start.2 = (f32[32,128]{1,0:T(8,128)S(1)}, f32[32,128]{1,0:T(8,128)S(1)}, u32[]{:S(2)}, u32[]{:S(2)}) collective-permute-start(f32[32,128]{1,0:T(8,128)S(1)} %shard_map.74.refs_0_), channel_id=1, source_target_pairs={{0,25},{1,24},{2,27},{3,26},{4,29},{5,28},{6,31},{7,30},{8,17},{9,... | collective-permute-start | bytes 49160 | tf_op jit(solution)/shard_map/ppermute | solution.py:349
  6.7 0.0 collective-permute-start.3
  6.7 0.6 %collective-permute-start.4 = (f32[32,128]{1,0:T(8,128)S(1)}, f32[32,128]{1,0:T(8,128)S(1)}, u32[]{:S(2)}, u32[]{:S(2)}) collective-permute-start(f32[32,128]{1,0:T(8,128)S(1)} %shard_map.74.refs_0_), channel_id=1, source_target_pairs={{0,8},{1,9},{2,10},{3,11},{4,12},{5,13},{6,14},{7,15},{8,0},{9,1},... | collective-permute-start | bytes 49160 | tf_op jit(solution)/shard_map/ppermute | solution.py:349
  7.4 0.8 %collective-permute-done.2.refs_1_ = f32[32,128]{1,0:T(8,128)S(1)} collective-permute-done((f32[32,128]{1,0:T(8,128)S(1)}, f32[32,128]{1,0:T(8,128)S(1)}, u32[]{:S(2)}, u32[]{:S(2)}) %collective-permute-start.2) | collective-permute-done | bytes 16416 | tf_op jit(solution)/shard_map/ppermute | solution.py:349
  8.2 2.6 %collective-permute-done.3.refs_2_ = f32[32,128]{1,0:T(8,128)S(1)} collective-permute-done((f32[32,128]{1,0:T(8,128)S(1)}, f32[32,128]{1,0:T(8,128)S(1)}, u32[]{:S(2)}, u32[]{:S(2)}) %collective-permute-start.3) | collective-permute-done | bytes 16416 | tf_op jit(solution)/shard_map/ppermute | solution.py:349
  10.8 0.0 collective-permute-done.4.refs_3_
  10.8 2.5 %collective-permute-start.5 = (f32[80,128]{1,0:T(8,128)S(1)}, f32[80,128]{1,0:T(8,128)S(1)}, u32[]{:S(2)}, u32[]{:S(2)}) collective-permute-start(f32[80,128]{1,0:T(8,128)S(1)} %shard_map.75.refs_0_.source_ref), channel_id=1, source_target_pairs={{0,6},{1,7},{2,4},{3,5},{4,2},{5,3},{6,0},{7,1},{8,14},{9,15},{10,... | collective-permute-start | bytes 122888 | tf_op jit(solution)/shard_map/ppermute | solution.py:349
  13.3 0.4 %collective-permute-start.6 = (f32[80,128]{1,0:T(8,128)S(1)}, f32[80,128]{1,0:T(8,128)S(1)}, u32[]{:S(2)}, u32[]{:S(2)}) collective-permute-start(f32[80,128]{1,0:T(8,128)S(1)} %shard_map.75.refs_0_.source_ref), channel_id=1, source_target_pairs={{0,5},{1,4},{2,7},{3,6},{4,1},{5,0},{6,3},{7,2},{8,13},{9,12},{10,... | collective-permute-start | bytes 122888 | tf_op jit(solution)/shard_map/ppermute | solution.py:349
  13.7 0.4 %collective-permute-start.7 = (f32[80,128]{1,0:T(8,128)S(1)}, f32[80,128]{1,0:T(8,128)S(1)}, u32[]{:S(2)}, u32[]{:S(2)}) collective-permute-start(f32[80,128]{1,0:T(8,128)S(1)} %shard_map.75.refs_0_.source_ref), channel_id=1, source_target_pairs={{0,3},{1,2},{2,1},{3,0},{4,7},{5,6},{6,5},{7,4},{8,11},{9,10},{10,... | collective-permute-start | bytes 122888 | tf_op jit(solution)/shard_map/ppermute | solution.py:349
  14.1 1.7 %collective-permute-done.5.refs_1_.source_ref = f32[80,128]{1,0:T(8,128)S(1)} collective-permute-done((f32[80,128]{1,0:T(8,128)S(1)}, f32[80,128]{1,0:T(8,128)S(1)}, u32[]{:S(2)}, u32[]{:S(2)}) %collective-permute-start.5) | collective-permute-done | bytes 40992 | tf_op jit(solution)/shard_map/ppermute | solution.py:349
  15.8 1.0 %collective-permute-done.6.refs_2_.side_ref = f32[80,128]{1,0:T(8,128)S(1)} collective-permute-done((f32[80,128]{1,0:T(8,128)S(1)}, f32[80,128]{1,0:T(8,128)S(1)}, u32[]{:S(2)}, u32[]{:S(2)}) %collective-permute-start.6) | collective-permute-done | bytes 40992 | tf_op jit(solution)/shard_map/ppermute | solution.py:349
  16.8 0.3 %collective-permute-done.7.refs_3_.near_ref = f32[80,128]{1,0:T(8,128)S(1)} collective-permute-done((f32[80,128]{1,0:T(8,128)S(1)}, f32[80,128]{1,0:T(8,128)S(1)}, u32[]{:S(2)}, u32[]{:S(2)}) %collective-permute-start.7) | collective-permute-done | bytes 40992 | tf_op jit(solution)/shard_map/ppermute | solution.py:349
  17.1 0.3 %collective-permute-start.8 = (f32[16,128]{1,0:T(8,128)S(1)}, f32[16,128]{1,0:T(8,128)S(1)}, u32[]{:S(2)}, u32[]{:S(2)}) collective-permute-start(f32[16,128]{1,0:T(8,128)S(1)} %shard_map.76.mine_ref), channel_id=1, source_target_pairs={{0,1},{1,0},{2,3},{3,2},{4,5},{5,4},{6,7},{7,6},{8,9},{9,8},{10,11... | collective-permute-start | bytes 24584 | tf_op jit(solution)/shard_map/ppermute | solution.py:349
  17.4 1.0 %shard_map.77 = (bf16[512,384]{1,0:T(8,128)(2,1)S(1)}, bf16[512,384]{1,0:T(8,128)(2,1)S(1)}, f32[3,64,128]{2,1,0:T(8,128)S(1)}, f32[8,128]{1,0:T(8,128)S(1)}, f3...) custom-call(f32[384,512]{1,0:T(8,128)S(1)} %get-tuple-element.19.mode_ref, ...), custom_call_target="tpu_custom_call" | custom-call | flops 5000000 | bytes 100000 | tf_op jit(solution)/shard_map/pallas_call | solution.py:330
  18.4 0.7 %shard_map.78.before_ref = f32[64,256]{1,0:T(8,128)S(1)} custom-call(f32[8,128]{1,0:T(8,128)S(1)} %get-tuple-element.24.centre_ref, f32[3,64,128]{2,1,0:T(8,128)S(1)} %get-tuple-element.25.target_ref, f32[80,128]{1,0:T(8,128)S(1)} %shard_map.75.refs_0_.source_ref), custom_call_target="tpu_custom_call" | custom-call | flops 20000000 | bytes 100000 | tf_op jit(solution)/shard_map/pallas_call | solution.py:330
  19.1 0.7 %shard_map.79.first_ref = f32[64,256]{1,0:T(8,128)S(1)} custom-call(f32[8,128]{1,0:T(8,128)S(1)} %get-tuple-element.24.centre_ref, f32[3,64,128]{2,1,0:T(8,128)S(1)} %get-tuple-element.25.target_ref, f32[80,128]{1,0:T(8,128)S(1)} %collective-permute-done.5.refs_1_.source_ref, f32[64,256]{1,0:T(8,128)S(1)} %shard_map.78.before_ref), custom_call_target="tpu_custom_call" | custom-call | flops 20000000 | bytes 100000 | tf_op jit(solution)/shard_map/pallas_call | solution.py:330
  19.8 1.3 %shard_map.80.rest_ref = f32[12,64]{1,0:T(8,128)S(1)} custom-call(f32[8,128]{1,0:T(8,128)S(1)} %get-tuple-element.24.centre_ref, f32[3,64,128]{2,1,0:T(8,128)S(1)} %get-tuple-element.25.target_ref, f32[80,128]{1,0:T(8,128)S(1)} %collective-permute-done.6.refs_2_.side_ref, f32[80,128]{1,0:T(8,128)S(1)} %collective-permute-done.7.refs_3_.near_ref, ...), custom_call_target="tpu_custom_call" | custom-call | flops 20000000 | bytes 100000 | tf_op jit(solution)/shard_map/pallas_call | solution.py:330
  21.1 0.0 collective-permute-done.8.other_ref
  21.1 1.0 %shard_map.81 = f32[2,3,2,64]{3,2,1,0:T(2,128)} custom-call(f32[16,128]{1,0:T(8,128)S(1)} %shard_map.76.mine_ref, f32[16,128]{1,0:T(8,128)S(1)} %collective-permute-done.8.other_ref, bf16[512,384]{1,0:T(8,128)(2,1)S(1)} %get-tuple-element.20.high_ref, bf16[512,384]{1,0:T(8,128)(2,1)S(1)} %get-tuple-element.21.low_ref, ...), custom_call_target="tpu_custom_call" | custom-call | flops 100000 | bytes 100000 | tf_op jit(solution)/shard_map/pallas_call | solution.py:330
  (2 shorter events, 0.0 us)
Async XLA Ops:
  0.0 2.0 %collective-permute-start = (f32[2,3,2,64]{3,2,1,0:T(2,128)}, f32[2,3,2,64]{3,2,1,0:T(2,128)S(1)}, u32[]{:S(2)}, u32[]{:S(2)}) collective-permute-start(f32[2,3,2,64]{3,2,1,0:T(2,128)} %bitcast.8), channel_id=1, source_target_pairs={{0,1},{1,0},{2,3},{3,2},{4,5},{5,4},{6,7},{7,6},{8,9},{9,8},{10,11... | collective-permute-start | bytes 9224 | tf_op jit(solution)/shard_map/ppermute | solution.py:349
  0.5 1.5 %collective-permute-start.1 = (f32[3,64]{1,0:T(4,128)}, f32[3,64]{1,0:T(4,128)S(1)}, u32[]{:S(2)}, u32[]{:S(2)}) collective-permute-start(f32[3,64]{1,0:T(4,128)} %place_hbm.1), channel_id=1, source_target_pairs={{0,1},{1,0},{2,3},{3,2},{4,5},{5,4},{6,7},{7,6},{8,9},{9,8},{10,11... | collective-permute-start | bytes 2312 | tf_op jit(solution)/shard_map/ppermute | solution.py:349
  2.0 6.1 %collective-permute-start.2 = (f32[32,128]{1,0:T(8,128)S(1)}, f32[32,128]{1,0:T(8,128)S(1)}, u32[]{:S(2)}, u32[]{:S(2)}) collective-permute-start(f32[32,128]{1,0:T(8,128)S(1)} %shard_map.74.refs_0_), channel_id=1, source_target_pairs={{0,25},{1,24},{2,27},{3,26},{4,29},{5,28},{6,31},{7,30},{8,17},{9,... | collective-permute-start | bytes 49160 | tf_op jit(solution)/shard_map/ppermute | solution.py:349
  6.7 4.1 %collective-permute-start.3 = (f32[32,128]{1,0:T(8,128)S(1)}, f32[32,128]{1,0:T(8,128)S(1)}, u32[]{:S(2)}, u32[]{:S(2)}) collective-permute-start(f32[32,128]{1,0:T(8,128)S(1)} %shard_map.74.refs_0_), channel_id=1, source_target_pairs={{0,17},{1,16},{2,19},{3,18},{4,21},{5,20},{6,23},{7,22},{8,25},{9,... | collective-permute-start | bytes 49160 | tf_op jit(solution)/shard_map/ppermute | solution.py:349
  6.7 4.1 %collective-permute-start.4 = (f32[32,128]{1,0:T(8,128)S(1)}, f32[32,128]{1,0:T(8,128)S(1)}, u32[]{:S(2)}, u32[]{:S(2)}) collective-permute-start(f32[32,128]{1,0:T(8,128)S(1)} %shard_map.74.refs_0_), channel_id=1, source_target_pairs={{0,8},{1,9},{2,10},{3,11},{4,12},{5,13},{6,14},{7,15},{8,0},{9,1},... | collective-permute-start | bytes 49160 | tf_op jit(solution)/shard_map/ppermute | solution.py:349
  10.8 5.0 %collective-permute-start.5 = (f32[80,128]{1,0:T(8,128)S(1)}, f32[80,128]{1,0:T(8,128)S(1)}, u32[]{:S(2)}, u32[]{:S(2)}) collective-permute-start(f32[80,128]{1,0:T(8,128)S(1)} %shard_map.75.refs_0_.source_ref), channel_id=1, source_target_pairs={{0,6},{1,7},{2,4},{3,5},{4,2},{5,3},{6,0},{7,1},{8,14},{9,15},{10,... | collective-permute-start | bytes 122888 | tf_op jit(solution)/shard_map/ppermute | solution.py:349
  13.3 3.5 %collective-permute-start.6 = (f32[80,128]{1,0:T(8,128)S(1)}, f32[80,128]{1,0:T(8,128)S(1)}, u32[]{:S(2)}, u32[]{:S(2)}) collective-permute-start(f32[80,128]{1,0:T(8,128)S(1)} %shard_map.75.refs_0_.source_ref), channel_id=1, source_target_pairs={{0,5},{1,4},{2,7},{3,6},{4,1},{5,0},{6,3},{7,2},{8,13},{9,12},{10,... | collective-permute-start | bytes 122888 | tf_op jit(solution)/shard_map/ppermute | solution.py:349
  13.7 3.4 %collective-permute-start.7 = (f32[80,128]{1,0:T(8,128)S(1)}, f32[80,128]{1,0:T(8,128)S(1)}, u32[]{:S(2)}, u32[]{:S(2)}) collective-permute-start(f32[80,128]{1,0:T(8,128)S(1)} %shard_map.75.refs_0_.source_ref), channel_id=1, source_target_pairs={{0,3},{1,2},{2,1},{3,0},{4,7},{5,6},{6,5},{7,4},{8,11},{9,10},{10,... | collective-permute-start | bytes 122888 | tf_op jit(solution)/shard_map/ppermute | solution.py:349
  17.1 4.0 %collective-permute-start.8 = (f32[16,128]{1,0:T(8,128)S(1)}, f32[16,128]{1,0:T(8,128)S(1)}, u32[]{:S(2)}, u32[]{:S(2)}) collective-permute-start(f32[16,128]{1,0:T(8,128)S(1)} %shard_map.76.mine_ref), channel_id=1, source_target_pairs={{0,1},{1,0},{2,3},{3,2},{4,5},{5,4},{6,7},{7,6},{8,9},{9,8},{10,11... | collective-permute-start | bytes 24584 | tf_op jit(solution)/shard_map/ppermute | solution.py:349
